TPU v7x, 8 devices: a whole 2x2x1 slice. The times are simulated.
8 devices in a mesh: fit: 1 (over z), comp: 2 (over y), data: 4 (over x, core).
Axes of the slice: x: 2, y: 2, z: 1, core: 2. Of those that a mesh axis runs over, the one named last changes fastest.
Arguments:
- points: bfloat16 [4096, 256], P(('fit', 'data'))
- mu_init: float32 [16384, 256], P(('fit', 'comp'))
- logpi_init: float32 [16384], P(('fit', 'comp'))
- inv_temp: float32 [3], replicated
Outputs:
- output 1: float32 [16384, 256], P(('fit', 'comp'))
- output 2: float32 [16384], P(('fit', 'comp'))
- output 3: float32 [4096], P(('fit', 'data'))
All inputs are finite; a program needn't handle non-finite values.
Results may differ from a plain program's by a relative error of at most 0.00129327.
Values are sent between devices in bfloat16 or wider.
A program may use at most 1 GiB of HBM per device.

v0:
```python
import jax
import jax.numpy as jnp
from jax import lax
from jax.sharding import PartitionSpec as P

EPS_COUNT = 1e-6
ALPHA = 1e-3


def solution(mesh):
    comp_size = mesh.shape["comp"]
    data_size = mesh.shape["data"]

    def local_fit(points, mu_init, logpi_init, inv_temp):
        total_rows = points.shape[0] * data_size
        total_comp = mu_init.shape[0] * comp_size
        norm_const = total_rows + total_comp * ALPHA
        row_sq = jnp.sum(jnp.square(points.astype(jnp.float32)), axis=1)
        mean_rows = mu_init
        log_w = logpi_init
        for sweep_idx in range(inv_temp.shape[0]):
            beta_t = inv_temp[sweep_idx]
            mean_sq = jnp.sum(mean_rows * mean_rows, axis=1)
            cross_dot = lax.dot_general(points, mean_rows.astype(jnp.bfloat16), (((1,), (1,)), ((), ())), preferred_element_type=jnp.float32)
            logits = log_w[None, :] - beta_t * (row_sq[:, None] - 2.0 * cross_dot + mean_sq[None, :])
            row_max = lax.pmax(jnp.max(logits, axis=1), "comp")
            shifted = jnp.exp(logits - row_max[:, None])
            row_sum = lax.psum(jnp.sum(shifted, axis=1), "comp")
            row_lse = row_max + jnp.log(row_sum)
            resp_rows = shifted / row_sum[:, None]
            counts = jnp.sum(resp_rows, axis=0)
            stat_sum = lax.dot_general(resp_rows.astype(jnp.bfloat16), points, (((0,), (0,)), ((), ())), preferred_element_type=jnp.float32)
            stat_sum, counts = lax.psum((stat_sum, counts), "data")
            mean_rows = stat_sum / (counts + EPS_COUNT)[:, None]
            log_w = jnp.log((counts + ALPHA) / norm_const)
        return mean_rows, log_w, row_lse

    row_spec = P(("fit", "data"), None)
    comp_spec = P(("fit", "comp"), None)
    weight_spec = P(("fit", "comp"))
    lse_spec = P(("fit", "data"))
    return jax.shard_map(local_fit, mesh=mesh, in_specs=(row_spec, comp_spec, weight_spec, P(None)), out_specs=(comp_spec, weight_spec, lse_spec), check_vma=False)
```

profile of v0, /device:TPU:0, one launch (start us, length us, event | category | flops | bytes accessed | tf_op | source)
XLA Modules:
  0.0 666.3 jit_solution(1073088431786493268)
XLA Ops:
  7.2 1.4 fusion.21
  8.6 1.3 multiply_reduce_fusion.3
  9.8 4.5 multiply_reduce_fusion.2
  14.4 19.0 %fusion.22 = (f32[1024]{0:T(1024)S(1)}, f32[1024,8192]{1,0:T(8,128)}) fusion(f32[8192]{0:T(1024)S(1)} %multiply_reduce_fusion.2, bf16[1024,256]{1,0:T(8,128)(2,1)} %param.4, f32[8192,256]{1,0:T(8,128)} %param.5, f32[1024]{0:T(1024)S(1)} %multiply_reduce_fusion.3, f32[]{:T(128)} %bitcast, f32[8192]{0:T(1024)} %param.6), kind=kOutput, calls=%fused_computation.39 | convolution fusion | flops 4347395072 | bytes 42541060 | tf_op jit(solution)/shard_map/dot_general | solution.py:24
  33.4 6.3 pmax.21
  39.6 13.6 %fusion.1 = f32[1024]{0:T(1024)S(1)} fusion(f32[1024,8192]{1,0:T(8,128)} %get-tuple-element.15, f32[1024]{0:T(1024)S(1)} %pmax.21), kind=kLoop, calls=%fused_computation.7 | loop fusion | flops 16776192 | bytes 33562624 | tf_op jit(solution)/shard_map/reduce_sum | solution.py:28
  53.3 5.1 psum.63
  58.3 14.3 %fusion.19 = (f32[8192]{0:T(1024)S(1)}, bf16[1024,8192]{1,0:T(8,128)(2,1)S(1)}) fusion(f32[1024]{0:T(1024)S(1)} %psum.63, f32[1024,8192]{1,0:T(8,128)} %get-tuple-element.15, f32[1024]{0:T(1024)S(1)} %pmax.21), kind=kLoop, calls=%fused_computation.37 | loop fusion | flops 33546240 | bytes 50372608 | tf_op jit(solution)/shard_map/reduce_sum | solution.py:31
  72.7 7.0 %fusion.10 = f32[8192,256]{1,0:T(8,128)} fusion(bf16[1024,256]{1,0:T(8,128)(2,1)S(1)} %copy-done, bf16[1024,8192]{1,0:T(8,128)(2,1)S(1)} %get-tuple-element.4), kind=kOutput, calls=%fused_computation.16 | convolution fusion | flops 4294967296 | bytes 25690112 | tf_op jit(solution)/shard_map/dot_general | solution.py:32
  79.7 11.1 %psum.64 = f32[8192]{0:T(1024)S(1)} all-reduce(f32[8192]{0:T(1024)S(1)} %get-tuple-element.3), channel_id=1, replica_groups=mesh['fit'=1,'comp'=2,'data'=4] {'data'}, use_global_device_ids=true, to_apply=%region_7.0 | all-reduce | flops 8192 | bytes 65536 | tf_op jit(solution)/shard_map/psum | solution.py:33
  90.9 137.9 %all-reduce.4.cloned.1.call-done = f32[8192,256]{1,0:T(8,128)} async-done(((f32[8192,256]{1,0:T(8,128)}), f32[8192,256]{1,0:T(8,128)}) %all-reduce.4.cloned.1.call-update) | async-done | bytes 8388624 | tf_op jit(solution)/shard_map/psum | solution.py:33
  228.8 4.6 multiply_reduce_fusion.1
  233.4 17.7 %fusion.23 = (f32[1024]{0:T(1024)S(1)}, f32[8192,1024]{1,0:T(8,128)}) fusion(f32[8192]{0:T(1024)S(1)} %multiply_reduce_fusion.1, bf16[1024,256]{1,0:T(8,128)(2,1)S(1)} %copy-done, f32[8192,256]{1,0:T(8,128)} %all-reduce.4.cloned.1.call-done, f32[8192]{0:T(1024)S(1)} %get-tuple-element.9, f32[1024]{0:T(1024)S(1)} %multiply_reduce_fusion.3, f32[]{:T(128)} %bitcast.1, ...), kind=kOutput, calls=%fused_computation.40 | convolution fusion | flops 4349492224 | bytes 42573828 | tf_op jit(solution)/shard_map/dot_general | solution.py:24
  251.2 4.9 pmax.22
  256.1 15.0 %fusion.2 = f32[1024]{0:T(1024)S(1)} fusion(f32[8192,1024]{1,0:T(8,128)} %get-tuple-element.17, f32[1024]{0:T(1024)S(1)} %pmax.22), kind=kLoop, calls=%fused_computation.8 | loop fusion | flops 16776192 | bytes 33562624 | tf_op jit(solution)/shard_map/reduce_sum | solution.py:28
  271.1 4.9 psum.66
  276.1 17.1 %fusion.8 = f32[8192,256]{1,0:T(8,128)} fusion(bf16[1024,256]{1,0:T(8,128)(2,1)S(1)} %copy-done, f32[8192,1024]{1,0:T(8,128)} %get-tuple-element.17, f32[1024]{0:T(1024)S(1)} %psum.66, f32[1024]{0:T(1024)S(1)} %pmax.22), kind=kOutput, calls=%fused_computation.14 | convolution fusion | flops 4320133120 | bytes 42475520 | tf_op jit(solution)/shard_map/dot_general | solution.py:32
  293.2 15.3 %fusion.14 = f32[8192]{0:T(1024)S(1)} fusion(f32[1024]{0:T(1024)S(1)} %psum.66, f32[8192,1024]{1,0:T(8,128)} %get-tuple-element.17, f32[1024]{0:T(1024)S(1)} %pmax.22), kind=kLoop, calls=%fused_computation.19 | loop fusion | flops 25157632 | bytes 33595392 | tf_op jit(solution)/shard_map/reduce_sum | solution.py:31
  308.6 11.9 %psum.67 = f32[8192]{0:T(1024)S(1)} all-reduce(f32[8192]{0:T(1024)S(1)} %fusion.14), channel_id=1, replica_groups=mesh['fit'=1,'comp'=2,'data'=4] {'data'}, use_global_device_ids=true, to_apply=%region_15.0 | all-reduce | flops 8192 | bytes 65536 | tf_op jit(solution)/shard_map/psum | solution.py:33
  320.5 120.7 %all-reduce.6.cloned.1.call-done = f32[8192,256]{1,0:T(8,128)} async-done(((f32[8192,256]{1,0:T(8,128)}), f32[8192,256]{1,0:T(8,128)}) %all-reduce.6.cloned.1.call-update) | async-done | bytes 8388624 | tf_op jit(solution)/shard_map/psum | solution.py:33
  441.1 4.6 multiply_reduce_fusion
  445.8 17.9 %fusion.24 = (f32[1024]{0:T(1024)S(1)}, f32[8192,1024]{1,0:T(8,128)}) fusion(f32[8192]{0:T(1024)S(1)} %multiply_reduce_fusion, bf16[1024,256]{1,0:T(8,128)(2,1)S(1)} %copy-done, f32[8192,256]{1,0:T(8,128)} %all-reduce.6.cloned.1.call-done, f32[8192]{0:T(1024)S(1)} %get-tuple-element.7, f32[1024]{0:T(1024)S(1)} %multiply_reduce_fusion.3, f32[]{:T(128)} %bitcast.2, ...), kind=kOutput, calls=%fused_computation.41 | convolution fusion | flops 4349492224 | bytes 42573828 | tf_op jit(solution)/shard_map/dot_general | solution.py:24
  463.6 4.9 pmax.23
  468.6 15.0 %fusion.4 = f32[1024]{0:T(1024)S(1)} fusion(f32[8192,1024]{1,0:T(8,128)} %get-tuple-element.19, f32[1024]{0:T(1024)S(1)} %pmax.23), kind=kLoop, calls=%fused_computation.10 | loop fusion | flops 16776192 | bytes 33562624 | tf_op jit(solution)/shard_map/reduce_sum | solution.py:28
  483.6 4.9 psum.69
  488.5 17.1 %fusion.6 = f32[8192,256]{1,0:T(8,128)} fusion(bf16[1024,256]{1,0:T(8,128)(2,1)S(1)} %copy-done, f32[8192,1024]{1,0:T(8,128)} %get-tuple-element.19, f32[1024]{0:T(1024)S(1)} %psum.69, f32[1024]{0:T(1024)S(1)} %pmax.23), kind=kOutput, calls=%fused_computation.12 | convolution fusion | flops 4320133120 | bytes 42475520 | tf_op jit(solution)/shard_map/dot_general | solution.py:32
  505.6 15.3 %fusion.12 = f32[8192]{0:T(1024)S(1)} fusion(f32[1024]{0:T(1024)S(1)} %psum.69, f32[8192,1024]{1,0:T(8,128)} %get-tuple-element.19, f32[1024]{0:T(1024)S(1)} %pmax.23), kind=kLoop, calls=%fused_computation.18 | loop fusion | flops 25157632 | bytes 33595392 | tf_op jit(solution)/shard_map/reduce_sum | solution.py:31
  521.0 11.7 %psum.71 = f32[8192]{0:T(1024)S(1)} all-reduce(f32[8192]{0:T(1024)S(1)} %fusion.12), channel_id=1, replica_groups=mesh['fit'=1,'comp'=2,'data'=4] {'data'}, use_global_device_ids=true, to_apply=%region_24.0 | all-reduce | flops 8192 | bytes 65536 | tf_op jit(solution)/shard_map/psum | solution.py:33
  532.7 0.6 log_add_fusion
  533.3 0.6 multiply_log_fusion
  533.9 119.7 %all-reduce.8.cloned.1.call-done = f32[8192,256]{1,0:T(8,128)} async-done(((f32[8192,256]{1,0:T(8,128)}), f32[8192,256]{1,0:T(8,128)}) %all-reduce.8.cloned.1.call-update) | async-done | bytes 8388624 | tf_op jit(solution)/shard_map/psum | solution.py:33
  653.6 6.2 broadcast_divide_fusion
  (10 shorter events, 0.2 us)
Async XLA Ops:
  7.2 221.6 %all-reduce.4.cloned.1.call-start = ((), (), s32[]{:S(2)}) async-start(), calls=%async_computation | async-start | bytes 16777216 | tf_op jit(solution)/shard_map/psum | solution.py:33
  53.2 19.4 %copy-start = (bf16[1024,256]{1,0:T(8,128)(2,1)S(1)}, bf16[1024,256]{1,0:T(8,128)(2,1)}, u32[]{:S(2)}) copy-start(bf16[1024,256]{1,0:T(8,128)(2,1)} %param.4) | copy-start | bytes 1572868
  79.7 361.5 %all-reduce.6.cloned.1.call-start = ((), (), s32[]{:S(2)}) async-start(), calls=%async_computation.1 | async-start | bytes 16777216 | tf_op jit(solution)/shard_map/psum | solution.py:33
  293.2 360.4 %all-reduce.8.cloned.1.call-start = ((), (), s32[]{:S(2)}) async-start(), calls=%async_computation.2 | async-start | bytes 16777216 | tf_op jit(solution)/shard_map/psum | solution.py:33
Sparse Core Ops, SparseCore 0:
  79.8 148.9 all-reduce.3
  293.3 147.8 all-reduce.5
  505.8 147.8 all-reduce.7
where the time goes:
time: 668 us; the launch traced here: 666 us
  waiting for transfers between devices  378 us (57%)
  other arithmetic  111 us (17%)
  matrix products  95.7 us (14%)
  blocking collectives  65.7 us (10%)
  between operations  13.9 us (2%)
    psum x3, waiting for transfers between devices, local_fit(): stat_sum, counts = lax.psum((stat_sum, counts), 'data')  378 us
    dot_general x3, matrix products, local_fit(): lax.dot_general(points, mean_rows.astype(jnp.bfloat16), (((1,), (1,)), ((...  54.6 us
    reduce_sum x3, other arithmetic, local_fit(): counts = jnp.sum(resp_rows, axis=0)  44.9 us
    reduce_sum x3, other arithmetic, local_fit(): row_sum = lax.psum(jnp.sum(shifted, axis=1), 'comp')  43.7 us
    dot_general x3, matrix products, local_fit(): lax.dot_general(resp_rows.astype(jnp.bfloat16), points, (((0,), (0,)), ((...  41.1 us
    psum x3, blocking collectives, local_fit(): stat_sum, counts = lax.psum((stat_sum, counts), 'data')  34.7 us
    pmax x3, blocking collectives, local_fit(): row_max = lax.pmax(jnp.max(logits, axis=1), 'comp')  16.1 us
    psum x3, blocking collectives, local_fit(): row_sum = lax.psum(jnp.sum(shifted, axis=1), 'comp')  14.9 us
  transfers between devices with their start and end apart: 3, of which 3 were waited for; matrix products, arithmetic and copies ran while one was open for 5% of the time, Pallas kernels for 0%

commit v1 on v0

v1 whole, which is shorter than its diff:
```python
import jax
import jax.numpy as jnp
from jax import lax
from jax.sharding import PartitionSpec as P

EPS_COUNT = 1e-6
ALPHA = 1e-3


def solution(mesh):
    comp_size = mesh.shape["comp"]
    data_size = mesh.shape["data"]

    def local_fit(points, mu_init, logpi_init, inv_temp):
        total_rows = points.shape[0] * data_size
        total_comp = mu_init.shape[0] * comp_size
        norm_const = total_rows + total_comp * ALPHA
        pts = lax.all_gather(points, "data", axis=0, tiled=True)
        own = mu_init.shape[0] // data_size
        start = lax.axis_index("data") * own
        mean_rows = lax.dynamic_slice_in_dim(mu_init, start, own, 0)
        log_w = lax.dynamic_slice_in_dim(logpi_init, start, own, 0)
        row_sq = jnp.sum(jnp.square(pts.astype(jnp.float32)), axis=1)
        for sweep_idx in range(inv_temp.shape[0]):
            beta_t = inv_temp[sweep_idx]
            mean_sq = jnp.sum(mean_rows * mean_rows, axis=1)
            cross = lax.dot_general(mean_rows.astype(jnp.bfloat16), pts, (((1,), (1,)), ((), ())), preferred_element_type=jnp.float32)
            logits = log_w[:, None] - beta_t * (row_sq[None, :] - 2.0 * cross + mean_sq[:, None])
            m_loc = jnp.max(logits, axis=0)
            expd = jnp.exp(logits - m_loc[None, :])
            s_loc = jnp.sum(expd, axis=0)
            stats = lax.all_gather(jnp.stack([m_loc, s_loc]), ("comp", "data"), axis=0)
            row_max = jnp.max(stats[:, 0], axis=0)
            row_sum = jnp.sum(stats[:, 1] * jnp.exp(stats[:, 0] - row_max[None, :]), axis=0)
            row_lse = row_max + jnp.log(row_sum)
            resp = expd * jnp.exp(m_loc - row_lse)[None, :]
            counts = jnp.sum(resp, axis=1)
            stat_sum = lax.dot_general(resp.astype(jnp.bfloat16), pts, (((1,), (0,)), ((), ())), preferred_element_type=jnp.float32)
            mean_rows = stat_sum / (counts + EPS_COUNT)[:, None]
            log_w = jnp.log((counts + ALPHA) / norm_const)
        means = lax.all_gather(mean_rows, "data", axis=0, tiled=True)
        weights = lax.all_gather(log_w, "data", axis=0, tiled=True)
        n_pts = points.shape[0]
        lse = lax.dynamic_slice_in_dim(row_lse, lax.axis_index("data") * n_pts, n_pts, 0)
        return means, weights, lse

    row_spec = P(("fit", "data"), None)
    comp_spec = P(("fit", "comp"), None)
    weight_spec = P(("fit", "comp"))
    lse_spec = P(("fit", "data"))
    return jax.shard_map(local_fit, mesh=mesh, in_specs=(row_spec, comp_spec, weight_spec, P(None)), out_specs=(comp_spec, weight_spec, lse_spec), check_vma=False)
```

time: 668 us -> 297 us (0.44)
  waiting for transfers between devices: 378 us -> 67.8 us
  other arithmetic: 111 us -> 66.8 us
  blocking collectives: 65.7 us -> 44.7 us
  local copies, waits for them, and re-layouts: 1.36 us -> 10.6 us
    psum x3 -> x0, waiting for transfers between devices: 378 us -> none  [local_fit(): stat_sum, counts = lax.psum((stat_sum, counts), 'data')]
    all_gather x0 -> x2, waiting for transfers between devices: none -> 67.1 us  [the longest x1 47.2 us: local_fit(): means = lax.all_gather(mean_rows, 'data', axis=0, tiled=True)]
    psum x6 -> x0, blocking collectives: 49.7 us -> none  [the longest x3 34.7 us: local_fit(): stat_sum, counts = lax.psum((stat_sum, counts), 'data')]
    all_gather x0 -> x4, blocking collectives: none -> 44.7 us  [the longest x3 36.5 us: local_fit(): stats = lax.all_gather(jnp.stack([m_loc, s_loc]), ('comp', 'data'), axis=0)]
    reduce_sum x7 -> x10, other arithmetic: 89.9 us -> 64 us  [the longest x3 42.7 us: local_fit(): s_loc = jnp.sum(expd, axis=0)]
    pmax x3 -> x0, blocking collectives: 16.1 us -> none  [local_fit(): row_max = lax.pmax(jnp.max(logits, axis=1), 'comp')]
    reduce_sum x3 -> x1, other arithmetic: 13.8 us -> 1.93 us  [local_fit(): mean_sq = jnp.sum(mean_rows * mean_rows, axis=1)]
    unnamed x2 -> x10, local copies, waits for them, and re-layouts: 0.01 us -> 7.95 us
  transfers between devices with their start and end apart: 3 -> 2, of which waited for: 3 -> 2; matrix products, arithmetic and copies ran while one was open for 5% -> 2% of each run, Pallas kernels for 0% -> 0%
where the time goes in v1:
time: 297 us
  matrix products  92.8 us (31%)
  waiting for transfers between devices  67.8 us (23%)
  other arithmetic  66.8 us (22%)
  blocking collectives  44.7 us (15%)
  between operations  14.3 us (5%)
  local copies, waits for them, and re-layouts  10.6 us (4%)
    dot_general x3, matrix products, local_fit(): lax.dot_general(mean_rows.astype(jnp.bfloat16), pts, (((1,), (1,)), ((),...  50 us
    all_gather x1, waiting for transfers between devices, local_fit(): means = lax.all_gather(mean_rows, 'data', axis=0, tiled=True)  47.2 us
    dot_general x3, matrix products, local_fit(): lax.dot_general(resp.astype(jnp.bfloat16), pts, (((1,), (0,)), ((), ())),...  42.8 us
    reduce_sum x3, other arithmetic, local_fit(): s_loc = jnp.sum(expd, axis=0)  42.7 us
    all_gather x3, blocking collectives, local_fit(): stats = lax.all_gather(jnp.stack([m_loc, s_loc]), ('comp', 'data'), axis=0)  36.5 us
    all_gather x1, waiting for transfers between devices, local_fit(): pts = lax.all_gather(points, 'data', axis=0, tiled=True)  20 us
    reduce_sum x3, other arithmetic, local_fit(): counts = jnp.sum(resp, axis=1)  18.6 us
    all_gather x1, blocking collectives, local_fit(): weights = lax.all_gather(log_w, 'data', axis=0, tiled=True)  8.17 us
  transfers between devices with their start and end apart: 2, of which 2 were waited for; matrix products, arithmetic and copies ran while one was open for 2% of the time, Pallas kernels for 0%

profile of v1, /device:TPU:0, one launch (start us, length us, event | category | flops | bytes accessed | tf_op | source)
XLA Modules:
  0.0 297.1 jit_solution(12618313572594994615)
XLA Ops:
  7.2 0.7 all-gather.9.cloned.1.call-update
  7.9 0.7 dynamic_slice.9
  8.7 1.9 multiply_reduce_fusion.6
  10.6 1.4 fusion.24
  11.9 20.0 %all-gather.9.cloned.1.call-done = bf16[4096,256]{1,0:T(8,128)(2,1)} async-done(((bf16[1024,256]{1,0:T(8,128)(2,1)}), bf16[4096,256]{1,0:T(8,128)(2,1)}) %all-gather.9.cloned.1.call-update) | async-done | bytes 2097168 | tf_op jit(solution)/shard_map/all_gather | solution.py:18
  31.9 2.2 multiply_reduce_fusion.3
  34.1 17.1 %fusion.25 = (f32[4096]{0:T(1024)S(1)}, f32[2048,4096]{1,0:T(8,128)}) fusion(f32[2048]{0:T(1024)S(1)} %multiply_reduce_fusion.6, bf16[4096,256]{1,0:T(8,128)(2,1)} %all-gather.9.cloned.1.call-done, f32[8192,256]{1,0:T(8,128)} %param.5, s32[]{:T(128)S(6)} %select_n.7, f32[4096]{0:T(1024)S(1)} %multiply_reduce_fusion.3, f32[]{:T(128)} %bitcast, ...), kind=kOutput, calls=%fused_computation.64 | convolution fusion | flops 4345294848 | bytes 36749828 | tf_op jit(solution)/shard_map/dot_general | solution.py:27
  51.2 15.4 %fusion = f32[4096]{0:T(1024)S(1)} fusion(f32[2048,4096]{1,0:T(8,128)} %get-tuple-element.24, f32[4096]{0:T(1024)S(1)} %get-tuple-element.23), kind=kLoop, calls=%fused_computation.12 | loop fusion | flops 16773120 | bytes 33587200 | tf_op jit(solution)/shard_map/reduce_sum | solution.py:31
  66.7 12.1 %all-gather.3 = f32[8,2,4096]{2,1,0:T(2,128)S(1)} all-gather(f32[1,2,4096]{2,1,0:T(2,128)S(1)} %maximum_bitcast_fusion), channel_id=2, replica_groups=mesh['fit'=1,'comp'=2,'data'=4] {'comp','data'}, dimensions={0}, use_global_device_ids=true | all-gather | bytes 294912 | tf_op jit(solution)/shard_map/all_gather | solution.py:32
  78.8 0.2 fusion.23
  79.1 0.2 fusion.16
  79.3 6.2 %multiply_reduce_fusion.2 = f32[2048]{0:T(1024)S(1)} fusion(f32[2048,4096]{1,0:T(8,128)S(1)} %copy-done.1, f32[4096]{0:T(1024)S(1)} %subtract_exponential_fusion.5, f32[4096]{0:T(1024)S(1)} %get-tuple-element.23), kind=kLoop, calls=%fused_computation.11 | loop fusion | flops 25163776 | bytes 33595392 | tf_op jit(solution)/shard_map/reduce_sum | solution.py:37
  85.5 14.1 %multiply_reduce_fusion.5 = (f32[2048]{0:T(1024)S(1)}, bf16[2048,256]{0,1:T(8,128)(2,1)S(1)}) fusion(f32[2048]{0:T(1024)S(1)} %get-tuple-element.19, bf16[4096,256]{1,0:T(8,128)(2,1)S(1)} %copy-done.3, f32[2048,4096]{1,0:T(8,128)} %get-tuple-element.24, f32[4096]{0:T(1024)S(1)} %subtract_exponential_fusion.5, f32[4096]{0:T(1024)S(1)} %get-tuple-element.23), kind=kOutput, calls=%fused_computation.23 | convolution fusion | flops 4322228224 | bytes 36749312 | tf_op jit(solution)/shard_map/dot_general | solution.py:38
  99.6 16.5 %fusion.26 = (f32[4096]{0:T(1024)S(1)}, f32[2048,4096]{1,0:T(8,128)}) fusion(f32[2048]{0:T(1024)S(1)} %get-tuple-element.25, bf16[4096,256]{1,0:T(8,128)(2,1)S(1)} %copy-done.3, bf16[2048,256]{0,1:T(8,128)(2,1)S(1)} %get-tuple-element.26, f32[4096]{0:T(1024)S(1)} %multiply_reduce_fusion.3, f32[]{:T(128)} %bitcast.5, f32[2048]{0:T(1024)S(1)} %get-tuple-element.18), kind=kOutput, calls=%fused_computation.65 | convolution fusion | flops 4345294848 | bytes 36749316 | tf_op jit(solution)/shard_map/dot_general | solution.py:27
  116.1 13.6 %fusion.1 = f32[4096]{0:T(1024)S(1)} fusion(f32[2048,4096]{1,0:T(8,128)} %get-tuple-element.28, f32[4096]{0:T(1024)S(1)} %get-tuple-element.27), kind=kLoop, calls=%fused_computation.13 | loop fusion | flops 16773120 | bytes 33587200 | tf_op jit(solution)/shard_map/reduce_sum | solution.py:31
  129.7 12.2 %all-gather.4 = f32[8,2,4096]{2,1,0:T(2,128)S(1)} all-gather(f32[1,2,4096]{2,1,0:T(2,128)S(1)} %maximum_bitcast_fusion.1), channel_id=3, replica_groups=mesh['fit'=1,'comp'=2,'data'=4] {'comp','data'}, dimensions={0}, use_global_device_ids=true | all-gather | bytes 294912 | tf_op jit(solution)/shard_map/all_gather | solution.py:32
  141.9 0.2 fusion.22
  142.2 0.2 fusion.14
  142.4 6.2 %multiply_reduce_fusion.1 = f32[2048]{0:T(1024)S(1)} fusion(f32[2048,4096]{1,0:T(8,128)S(1)} %copy-done.2, f32[4096]{0:T(1024)S(1)} %subtract_exponential_fusion.4, f32[4096]{0:T(1024)S(1)} %get-tuple-element.27), kind=kLoop, calls=%fused_computation.9 | loop fusion | flops 25163776 | bytes 33595392 | tf_op jit(solution)/shard_map/reduce_sum | solution.py:37
  148.6 14.1 %multiply_reduce_fusion.4 = (f32[2048]{0:T(1024)S(1)}, bf16[2048,256]{0,1:T(8,128)(2,1)S(1)}) fusion(f32[2048]{0:T(1024)S(1)} %get-tuple-element.17, bf16[4096,256]{1,0:T(8,128)(2,1)S(1)} %copy-done.3, f32[2048,4096]{1,0:T(8,128)} %get-tuple-element.28, f32[4096]{0:T(1024)S(1)} %subtract_exponential_fusion.4, f32[4096]{0:T(1024)S(1)} %get-tuple-element.27), kind=kOutput, calls=%fused_computation.22 | convolution fusion | flops 4322228224 | bytes 36749312 | tf_op jit(solution)/shard_map/dot_general | solution.py:38
  162.7 16.5 %fusion.27 = (f32[4096]{0:T(1024)S(1)}, f32[2048,4096]{1,0:T(8,128)}) fusion(f32[2048]{0:T(1024)S(1)} %get-tuple-element.29, bf16[4096,256]{1,0:T(8,128)(2,1)S(1)} %copy-done.3, bf16[2048,256]{0,1:T(8,128)(2,1)S(1)} %get-tuple-element.30, f32[4096]{0:T(1024)S(1)} %multiply_reduce_fusion.3, f32[]{:T(128)} %bitcast.10, f32[2048]{0:T(1024)S(1)} %get-tuple-element.16), kind=kOutput, calls=%fused_computation.66 | convolution fusion | flops 4345294848 | bytes 36749316 | tf_op jit(solution)/shard_map/dot_general | solution.py:27
  179.1 13.6 %fusion.2 = f32[4096]{0:T(1024)S(1)} fusion(f32[2048,4096]{1,0:T(8,128)} %get-tuple-element.32, f32[4096]{0:T(1024)S(1)} %get-tuple-element.31), kind=kLoop, calls=%fused_computation.14 | loop fusion | flops 16773120 | bytes 33587200 | tf_op jit(solution)/shard_map/reduce_sum | solution.py:31
  192.8 12.2 %all-gather.5 = f32[8,2,4096]{2,1,0:T(2,128)S(1)} all-gather(f32[1,2,4096]{2,1,0:T(2,128)S(1)} %maximum_bitcast_fusion.2), channel_id=4, replica_groups=mesh['fit'=1,'comp'=2,'data'=4] {'comp','data'}, dimensions={0}, use_global_device_ids=true | all-gather | bytes 294912 | tf_op jit(solution)/shard_map/all_gather | solution.py:32
  205.0 0.2 fusion.21
  205.3 0.2 fusion.12
  205.5 6.2 %multiply_reduce_fusion = f32[2048]{0:T(1024)S(1)} fusion(f32[2048,4096]{1,0:T(8,128)S(1)} %copy-done, f32[4096]{0:T(1024)S(1)} %get-tuple-element.3, f32[4096]{0:T(1024)S(1)} %get-tuple-element.31), kind=kLoop, calls=%fused_computation.6 | loop fusion | flops 25163776 | bytes 33595392 | tf_op jit(solution)/shard_map/reduce_sum | solution.py:37
  211.7 14.6 %fusion.6 = f32[2048,256]{1,0:T(8,128)} fusion(bf16[4096,256]{1,0:T(8,128)(2,1)S(1)} %copy-done.3, f32[2048,4096]{1,0:T(8,128)} %get-tuple-element.32, f32[4096]{0:T(1024)S(1)} %get-tuple-element.3, f32[4096]{0:T(1024)S(1)} %get-tuple-element.31, f32[2048]{0:T(1024)S(1)} %get-tuple-element.15), kind=kOutput, calls=%fused_computation.19 | convolution fusion | flops 4320657408 | bytes 37789696 | tf_op jit(solution)/shard_map/dot_general | solution.py:38
  226.4 8.2 %all_gather.35 = f32[8192]{0:T(1024)S(1)} all-gather(f32[2048]{0:T(1024)S(1)} %get-tuple-element.14), channel_id=1, replica_groups=mesh['fit'=1,'comp'=2,'data'=4] {'data'}, dimensions={0}, use_global_device_ids=true | all-gather | bytes 40960 | tf_op jit(solution)/shard_map/all_gather | solution.py:42
  234.5 0.6 dynamic_slice.11
  235.1 47.2 %all-gather.11.cloned.1.call-done = f32[8192,256]{1,0:T(8,128)} async-done(((f32[2048,256]{1,0:T(8,128)}), f32[8192,256]{1,0:T(8,128)}) %all-gather.11.cloned.1.call-update) | async-done | bytes 8388624 | tf_op jit(solution)/shard_map/all_gather | solution.py:41
  282.3 7.3 %copy.39 = f32[8192,256]{1,0:T(8,128)} copy(f32[8192,256]{1,0:T(8,128)} %all-gather.11.cloned.1.call-done) | data formatting | bytes 16777216
  289.6 0.6 copy.40
  (20 shorter events, 0.3 us)
Async XLA Ops:
  7.2 24.7 %all-gather.9.cloned.1.call-start = ((), (), s32[]{:S(2)}) async-start(), calls=%async_computation | async-start | bytes 2621440 | tf_op jit(solution)/shard_map/all_gather | solution.py:18
  7.9 274.4 %all-gather.11.cloned.1.call-start = ((), (), s32[]{:S(2)}) async-start(), calls=%async_computation.1 | async-start | bytes 10485760 | tf_op jit(solution)/shard_map/all_gather | solution.py:41
  51.2 28.1 %copy-start.1 = (f32[2048,4096]{1,0:T(8,128)S(1)}, f32[2048,4096]{1,0:T(8,128)}, u32[]{:S(2)}) copy-start(f32[2048,4096]{1,0:T(8,128)} %get-tuple-element.24) | copy-start | bytes 100663296
  51.2 34.3 %copy-start.3 = (bf16[4096,256]{1,0:T(8,128)(2,1)S(1)}, bf16[4096,256]{1,0:T(8,128)(2,1)}, u32[]{:S(2)}) copy-start(bf16[4096,256]{1,0:T(8,128)(2,1)} %all-gather.9.cloned.1.call-done) | copy-start | bytes 6291460
  116.1 26.3 %copy-start.2 = (f32[2048,4096]{1,0:T(8,128)S(1)}, f32[2048,4096]{1,0:T(8,128)}, u32[]{:S(2)}) copy-start(f32[2048,4096]{1,0:T(8,128)} %get-tuple-element.28) | copy-start | bytes 100663296
  179.1 26.4 %copy-start = (f32[2048,4096]{1,0:T(8,128)S(1)}, f32[2048,4096]{1,0:T(8,128)}, u32[]{:S(2)}) copy-start(f32[2048,4096]{1,0:T(8,128)} %get-tuple-element.32) | copy-start | bytes 100663296
Sparse Core Ops, SparseCore 0:
  9.5 22.3 all-gather.8
  226.5 55.7 all-gather.10

commit v2 on v0

v2 whole, which is shorter than its diff:
```python
import functools
import math

import jax
import jax.numpy as jnp
from jax import lax
from jax.experimental import pallas as pl
from jax.experimental.pallas import tpu as pltpu
from jax.sharding import PartitionSpec as P

EPS_COUNT = 1e-6
ALPHA = 1e-3
LOG2E = math.log2(math.e)
LN2 = math.log(2.0)
KB = 512
IB = 256
KT = 128
MESH = pl.DeviceIdType.MESH
F32 = jnp.float32
BF16 = jnp.bfloat16
NT = (((1,), (1,)), ((), ()))


def fit_kernel(cfg, temp_ref, pts_ref, mu_ref, logpi_ref, means_ref, logw_ref, lse_out_ref,
               x_ref, p_ref, mub_ref, muf_ref, c_ref, crow_ref, cfrow_ref, s_ref, n_ref, fin_ref,
               wrow_ref, m_ref, sum_ref, lse_ref, g_ref, lseo_ref,
               loc_sem, pts_send, pts_recv, st_send, st_recv, mu_send, mu_recv,
               out_loc, out_send, out_recv, w_loc, w_send, w_recv):
    sweeps, own, nq, dim, norm_const = cfg
    n_kb = own // KB
    n_kt = own // KT
    half = nq // 2
    fit = lax.axis_index("fit")
    comp = lax.axis_index("comp")
    data = lax.axis_index("data")
    xpos = data // 2

    def data_xor(d):
        if d == 0:
            return data
        if d == 1:
            return data + 1 - 2 * (data % 2)
        if d == 2:
            return (data + 2) % 4
        return (data + 1 - 2 * (data % 2) + 2) % 4

    def peer(r):
        return (fit, (comp + r // 4) % 2, data_xor(r % 4))

    sib, par = data_xor(1), data_xor(2)
    me = comp * 4 + data

    barrier = pltpu.get_barrier_semaphore()
    for r in range(1, 8):
        pl.semaphore_signal(barrier, inc=1, device_id=peer(r), device_id_type=MESH)

    ld_pts = pltpu.make_async_copy(pts_ref, x_ref.at[pl.ds(pl.multiple_of(data * nq, nq), nq)], loc_sem.at[0])
    ld_mu = pltpu.make_async_copy(mu_ref.at[pl.ds(pl.multiple_of(data * own, own), own)], s_ref, loc_sem.at[1])
    ld_pi = pltpu.make_async_copy(logpi_ref.at[data], crow_ref, loc_sem.at[2])
    ld_pts.start()
    ld_mu.start()
    ld_pi.start()
    pl.semaphore_wait(barrier, 7)

    def pts_copy(kind, ch):
        owner = data if kind < 2 else par
        rows = pl.ds(pl.multiple_of(owner * nq + ch * half, half), half)
        src = pts_ref.at[pl.ds(ch * half, half)] if kind < 2 else x_ref.at[rows]
        dev = peer(2) if kind == 1 else peer(1)
        return pltpu.make_async_remote_copy(
            src_ref=src, dst_ref=x_ref.at[rows], send_sem=pts_send.at[kind, ch], recv_sem=pts_recv.at[kind, ch],
            device_id=dev, device_id_type=MESH)

    for ch in range(2):
        pts_copy(1, ch).start()
    for ch in range(2):
        pts_copy(0, ch).start()

    def to_col(row):
        return jnp.transpose(jnp.broadcast_to(row, (128, row.shape[1])))

    def to_row(col):
        return jnp.transpose(col)[0:1, :]

    ld_pi.wait()
    ld_mu.wait()
    beta0 = temp_ref[0]

    def init_body(kb, _):
        rows = pl.ds(pl.multiple_of(kb * KB, KB), KB)
        mu = s_ref[rows, :]
        mub_ref[rows, :] = mu.astype(BF16)
        msq = jnp.sum(mu * mu, axis=1, keepdims=True)
        lp = to_col(crow_ref[:, rows])
        c_ref[rows, :] = LOG2E * (lp - beta0 * msq)
        return 0

    lax.fori_loop(0, n_kb, init_body, 0)

    def e_quarter(q, tb):
        for it in range(nq // IB):
            i0 = q * nq + it * IB
            xt = x_ref[pl.ds(pl.multiple_of(i0, IB), IB), :]
            for kb in range(n_kb):
                a = lax.dot_general(mub_ref[pl.ds(kb * KB, KB), :], xt, NT, preferred_element_type=F32)
                for u in range(KB // KT):
                    rows = pl.ds(kb * KB + u * KT, KT)
                    tile = kb * (KB // KT) + u
                    cc = c_ref[rows, :]
                    for lc in range(IB // 128):
                        cols = pl.ds(pl.multiple_of(i0 + lc * 128, 128), 128)
                        l = a[u * KT:(u + 1) * KT, lc * 128:(lc + 1) * 128] * tb + cc
                        l3 = l.reshape(KT // 8, 8, 128)
                        m = jnp.max(l3, axis=0)
                        p3 = jnp.exp2(l3 - m[None])
                        p_ref[rows, cols] = p3.reshape(KT, 128)
                        m_ref[tile, :, cols] = m
                        sum_ref[tile, :, pl.ds(it * IB + lc * 128, 128)] = jnp.sum(p3, axis=0)

    def st_copy(t, q, r):
        return pltpu.make_async_remote_copy(
            src_ref=g_ref.at[t, q, me], dst_ref=g_ref.at[t, q, me], send_sem=st_send.at[t, q, r],
            recv_sem=st_recv.at[t, q, r], device_id=peer(r), device_id_type=MESH)

    def st_send_all(t, q):
        cols = pl.ds(pl.multiple_of(q * nq, nq), nq)
        top = jnp.max(functools.reduce(jnp.maximum, [m_ref[k, :, cols] for k in range(n_kt)]), axis=0, keepdims=True)
        tot = functools.reduce(lambda u, v: u + v,
                               [sum_ref[k] * jnp.exp2(m_ref[k, :, cols] - top) for k in range(n_kt)])
        tot = jnp.sum(tot, axis=0, keepdims=True)
        g_ref[t, q, me] = top + LOG2E * jnp.log(tot)
        for r in range(1, 8):
            st_copy(t, q, r).start()

    def e_step(t, q, tb):
        e_quarter(q, tb)
        st_send_all(t, q)

    def st_combine(t, q):
        for r in range(1, 8):
            st_copy(t, q, r).wait_recv()
        cols = pl.ds(pl.multiple_of(q * nq, nq), nq)
        vals = [g_ref[t, q, s] for s in range(8)]
        top = functools.reduce(jnp.maximum, vals)
        tot = functools.reduce(lambda u, v: u + v, [jnp.exp2(v - top) for v in vals])
        lse = top + LOG2E * jnp.log(tot)
        lse_ref[:, cols] = lse
        for k in range(n_kt):
            m_ref[k, :, cols] = jnp.exp2(m_ref[k, :, cols] - lse)

    def m_block(kb, quarters):
        k0 = kb * KB
        ns = [jnp.zeros((KT, 128), F32)] * (KB // KT)
        acc = jnp.zeros((KB, dim), F32)
        for q in quarters:
            for ic in range(nq // IB):
                i0 = q * nq + ic * IB
                parts = []
                for u in range(KB // KT):
                    rows = pl.ds(pl.multiple_of(k0 + u * KT, KT), KT)
                    cols = pl.ds(i0, IB)
                    sc = m_ref[kb * (KB // KT) + u, :, cols]
                    r = (p_ref[rows, cols].reshape(KT // 8, 8, IB) * sc[None]).reshape(KT, IB)
                    ns[u] = ns[u] + (r[:, :128] + r[:, 128:])
                    parts.append(r.astype(BF16))
                rb = jnp.concatenate(parts, axis=0)
                acc = acc + jnp.dot(rb, x_ref[pl.ds(i0, IB), :], preferred_element_type=F32)
        return jnp.concatenate(ns, axis=0), acc

    def m_first(kb, _):
        rows = pl.ds(pl.multiple_of(kb * KB, KB), KB)
        n_acc, acc = m_block(kb, (0, 2))
        n_ref[rows, :] = n_acc
        s_ref[rows, :] = acc
        return 0

    def finish(n_acc, acc):
        n = jnp.sum(n_acc, axis=1, keepdims=True)
        mu = acc * (1.0 / (n + EPS_COUNT))
        return n, mu

    def mu_copy(kb):
        rows = pl.ds(pl.multiple_of(kb * KB, KB), KB)
        return pltpu.make_async_remote_copy(
            src_ref=mub_ref.at[rows], dst_ref=muf_ref.at[rows], send_sem=mu_send.at[kb], recv_sem=mu_recv.at[kb],
            device_id=peer(2), device_id_type=MESH)

    def c_copy():
        return pltpu.make_async_remote_copy(
            src_ref=crow_ref, dst_ref=cfrow_ref, send_sem=mu_send.at[n_kb], recv_sem=mu_recv.at[n_kb],
            device_id=peer(2), device_id_type=MESH)

    def m_second(kb, beta_next, share):
        rows = pl.ds(pl.multiple_of(kb * KB, KB), KB)
        n_acc, acc = m_block(kb, (1, 3))
        n, mu = finish(n_ref[rows, :] + n_acc, s_ref[rows, :] + acc)
        mub_ref[rows, :] = mu.astype(BF16)
        msq = jnp.sum(mu * mu, axis=1, keepdims=True)
        lp = jnp.log((jnp.broadcast_to(n, (KB, 128)) + ALPHA) / norm_const)
        c = LOG2E * (lp - beta_next * msq)
        c_ref[rows, :] = c
        if share:
            crow_ref[:, rows] = to_row(c)
            mu_copy(kb).start()

    def out_copies(slot, kb):
        owner = data if slot == 0 else par
        dst = means_ref.at[pl.ds(pl.multiple_of(owner * own + kb * KB, KB), KB)]
        src = fin_ref.at[slot, pl.ds(pl.multiple_of(kb * KB, KB), KB)]
        here = pltpu.make_async_copy(src, dst, out_loc.at[slot, kb])
        there = pltpu.make_async_remote_copy(
            src_ref=src, dst_ref=dst, send_sem=out_send.at[slot, kb], recv_sem=out_recv.at[slot, kb],
            device_id=peer(1), device_id_type=MESH)
        return here, there

    def w_copies(slot):
        owner = data if slot == 0 else par
        here = pltpu.make_async_copy(wrow_ref.at[slot], logw_ref.at[owner], w_loc.at[slot])
        there = pltpu.make_async_remote_copy(
            src_ref=wrow_ref.at[slot], dst_ref=logw_ref.at[owner], send_sem=w_send.at[slot], recv_sem=w_recv.at[slot],
            device_id=peer(1), device_id_type=MESH)
        return here, there

    def emit(slot, kb, n_acc, acc):
        rows = pl.ds(pl.multiple_of(kb * KB, KB), KB)
        n, mu = finish(n_acc, acc)
        fin_ref[slot, rows, :] = mu
        nrow = to_row(jnp.broadcast_to(n, (KB, 128)))
        wrow_ref[slot, :, rows] = jnp.log((nrow + ALPHA) / norm_const)
        for cp in out_copies(slot, kb):
            cp.start()

    for t in range(sweeps):
        beta = temp_ref[t]
        tb = (2.0 * LOG2E) * beta
        last = t == sweeps - 1
        if t == 0:
            ld_pts.wait()
            for ch in range(2):
                pts_copy(0, ch).wait_recv()
            lax.fori_loop(0, 2, lambda s, _: (e_step(0, xpos * 2 + s, tb), 0)[1], 0)
            for ch in range(2):
                pts_copy(1, ch).wait_recv()
                pts_copy(2, ch).start()
            for ch in range(2):
                pts_copy(2, ch).wait_recv()
            lax.fori_loop(0, 2, lambda s, _: (e_step(0, (1 - xpos) * 2 + s, tb), 0)[1], 0)
        else:
            lax.fori_loop(0, 4, lambda s, _: (e_step(t, (s % 2) * 2 + s // 2, tb), 0)[1], 0)
        st_combine(t, 0)
        st_combine(t, 2)
        lax.fori_loop(0, n_kb, m_first, 0)
        st_combine(t, 1)
        st_combine(t, 3)
        if not last:
            beta_next = temp_ref[t + 1]
            share = t == sweeps - 2
            lax.fori_loop(0, n_kb, lambda kb, _: (m_second(kb, beta_next, share), 0)[1], 0)
            if share:
                c_copy().start()
        else:
            def m_last(kb, _):
                rows = pl.ds(pl.multiple_of(kb * KB, KB), KB)
                n_acc, acc = m_block(kb, (1, 3))
                emit(0, kb, n_ref[rows, :] + n_acc, s_ref[rows, :] + acc)
                return 0

            lax.fori_loop(0, n_kb, m_last, 0)
            for cp in w_copies(0):
                cp.start()
            c_copy().wait_recv()

            def far_block(kb, _):
                mu_copy(kb).wait_recv()
                rows = pl.ds(pl.multiple_of(kb * KB, KB), KB)
                c = to_col(cfrow_ref[:, rows])
                c_ref[rows, :] = c
                n_ref[rows, :] = jnp.zeros((KB, 128), F32)
                s_ref[rows, :] = jnp.zeros((KB, dim), F32)

                def far_quarter(q, _):
                    cc = c_ref[rows, :]
                    c2 = jnp.concatenate([cc, cc], axis=1)
                    n_acc = n_ref[rows, :]
                    acc = s_ref[rows, :]
                    for ic in range(nq // IB):
                        cols = pl.ds(pl.multiple_of(q * nq + ic * IB, IB), IB)
                        xt = x_ref[cols, :]
                        a = lax.dot_general(muf_ref[rows, :], xt, NT, preferred_element_type=F32)
                        r = jnp.exp2((a * tb + c2) - lse_ref[:, cols])
                        n_acc = n_acc + (r[:, :128] + r[:, 128:])
                        acc = acc + jnp.dot(r.astype(BF16), xt, preferred_element_type=F32)
                    n_ref[rows, :] = n_acc
                    s_ref[rows, :] = acc
                    return 0

                lax.fori_loop(0, 4, far_quarter, 0)
                emit(1, kb, n_ref[rows, :], s_ref[rows, :])
                return 0

            lax.fori_loop(0, n_kb, far_block, 0)
            for cp in w_copies(1):
                cp.start()
            mine = pl.ds(pl.multiple_of(data * nq, nq), nq)
            xo = x_ref[mine, :].astype(F32)
            sq = xo * xo
            hi = sq.astype(BF16)
            lo = (sq - hi.astype(F32)).astype(BF16)
            ones = jnp.ones((8, dim), BF16)
            row_sq = (lax.dot_general(ones, hi, NT, preferred_element_type=F32)
                      + lax.dot_general(ones, lo, NT, preferred_element_type=F32))
            lseo_ref[...] = LN2 * lse_ref[:, mine] - beta * row_sq[0:1, :]
            lse_cp = pltpu.make_async_copy(lseo_ref, lse_out_ref, loc_sem.at[3])
            lse_cp.start()
            lse_cp.wait()

    for kind in range(3):
        for ch in range(2):
            pts_copy(kind, ch).wait_send()
    for t in range(sweeps):
        for q in range(4):
            for r in range(1, 8):
                st_copy(t, q, r).wait_send()
    for kb in range(n_kb):
        mu_copy(kb).wait_send()
    c_copy().wait_send()
    for slot in range(2):
        for kb in range(n_kb):
            here, there = out_copies(slot, kb)
            here.wait()
            there.wait_send()
        here, there = w_copies(slot)
        here.wait()
        there.wait_send()
    for slot in range(2):
        sib_slot_recv(slot, means_ref, logw_ref, out_copies, w_copies, n_kb)


def sib_slot_recv(slot, means_ref, logw_ref, out_copies, w_copies, n_kb):
    for kb in range(n_kb):
        out_copies(slot, kb)[1].wait_recv()
    w_copies(slot)[1].wait_recv()


def solution(mesh):
    comp_size = mesh.shape["comp"]
    data_size = mesh.shape["data"]

    def local_fit(points, mu_init, logpi_init, inv_temp):
        nq, dim = points.shape
        rows = mu_init.shape[0]
        own = rows // data_size
        sweeps = inv_temp.shape[0]
        n_pts = nq * data_size
        n_kb = own // KB
        norm_const = n_pts + rows * comp_size * ALPHA
        cfg = (sweeps, own, nq, dim, norm_const)
        any_spec = pl.BlockSpec(memory_space=pl.ANY)
        dma = pltpu.SemaphoreType.DMA
        means, logw, lse = pl.pallas_call(
            functools.partial(fit_kernel, cfg),
            out_shape=(jax.ShapeDtypeStruct((rows, dim), F32),
                       jax.ShapeDtypeStruct((data_size, 1, own), F32),
                       jax.ShapeDtypeStruct((1, nq), F32)),
            in_specs=[pl.BlockSpec(memory_space=pltpu.SMEM), any_spec, any_spec, any_spec],
            out_specs=(any_spec, any_spec, any_spec),
            scratch_shapes=[
                pltpu.VMEM((n_pts, dim), BF16),
                pltpu.VMEM((own, n_pts), F32),
                pltpu.VMEM((own, dim), BF16),
                pltpu.VMEM((own, dim), BF16),
                pltpu.VMEM((own, 128), F32),
                pltpu.VMEM((1, own), F32),
                pltpu.VMEM((1, own), F32),
                pltpu.VMEM((own, dim), F32),
                pltpu.VMEM((own, 128), F32),
                pltpu.VMEM((2, own, dim), F32),
                pltpu.VMEM((2, 1, own), F32),
                pltpu.VMEM((own // KT, 8, n_pts), F32),
                pltpu.VMEM((own // KT, 8, nq), F32),
                pltpu.VMEM((1, n_pts), F32),
                pltpu.VMEM((sweeps, data_size, 8, 1, nq), F32),
                pltpu.VMEM((1, nq), F32),
                dma((4,)),
                dma((3, 2)), dma((3, 2)),
                dma((sweeps, 4, 8)), dma((sweeps, 4, 8)),
                dma((n_kb + 1,)), dma((n_kb + 1,)),
                dma((2, n_kb)), dma((2, n_kb)), dma((2, n_kb)),
                dma((2,)), dma((2,)), dma((2,)),
            ],
            compiler_params=pltpu.CompilerParams(
                collective_id=0, has_side_effects=True, vmem_limit_bytes=62 * 1024 * 1024),
        )(inv_temp, points, mu_init, logpi_init.reshape(data_size, 1, own))
        return means, logw.reshape(rows), lse.reshape(nq)

    row_spec = P(("fit", "data"), None)
    comp_spec = P(("fit", "comp"), None)
    weight_spec = P(("fit", "comp"))
    lse_spec = P(("fit", "data"))
    return jax.shard_map(local_fit, mesh=mesh, in_specs=(row_spec, comp_spec, weight_spec, P(None)), out_specs=(comp_spec, weight_spec, lse_spec), check_vma=False)
```

time: 668 us -> 111 us (0.17)
  waiting for transfers between devices: 378 us -> 0 us
  other arithmetic: 111 us -> 0 us
  Pallas kernels: 0 us -> 101 us
  matrix products: 95.7 us -> 0 us
  blocking collectives: 65.7 us -> 0 us
  between operations: 13.9 us -> 0.66 us
  local copies, waits for them, and re-layouts: 1.36 us -> 8.54 us
    psum x3 -> x0, waiting for transfers between devices: 378 us -> none  [local_fit(): stat_sum, counts = lax.psum((stat_sum, counts), 'data')]
    reduce_sum x10 -> x0, other arithmetic: 104 us -> none  [the longest x3 44.9 us: local_fit(): counts = jnp.sum(resp_rows, axis=0)]
    pallas_call x0 -> x1, Pallas kernels: none -> 101 us  [local_fit(): pl.pallas_call(functools.partial(fit_kernel, cfg), out_shape=(jax.ShapeDt...]
    dot_general x6 -> x0, matrix products: 95.7 us -> none  [the longest x3 54.6 us: local_fit(): lax.dot_general(points, mean_rows.astype(jnp.bfloat16), (((1,), (1,)), ((...]
    psum x6 -> x0, blocking collectives: 49.7 us -> none  [the longest x3 34.7 us: local_fit(): stat_sum, counts = lax.psum((stat_sum, counts), 'data')]
    pmax x3 -> x0, blocking collectives: 16.1 us -> none  [local_fit(): row_max = lax.pmax(jnp.max(logits, axis=1), 'comp')]
    unnamed x2 -> x7, local copies, waits for them, and re-layouts: 0.01 us -> 8.54 us
  transfers between devices with their start and end apart: 3 -> 0, of which waited for: 3 -> 0; matrix products, arithmetic and copies ran while one was open for 5% -> 0% of each run, Pallas kernels for 0% -> 0%
where the time goes in v2:
time: 111 us; the launch traced here: 110 us
  Pallas kernels  101 us (91%)
  local copies, waits for them, and re-layouts  8.54 us (8%)
    pallas_call x1, Pallas kernels, local_fit(): pl.pallas_call(functools.partial(fit_kernel, cfg), out_shape=(jax.ShapeDt...  101 us
    unnamed x7, local copies, waits for them, and re-layouts  8.54 us

profile of v2, /device:TPU:0, one launch (start us, length us, event | category | flops | bytes accessed | tf_op | source)
XLA Modules:
  0.0 110.4 jit_solution(911929257843579756)
XLA Ops:
  0.6 101.2 %shard_map.67 = (f32[8192,256]{1,0:T(8,128)}, f32[4,1,2048]{2,1,0:T(1,128)}, f32[1,1024]{1,0:T(1,128)}) custom-call(f32[3]{0:T(128)} %temp_ref.1, bf16[1024,256]{1,0:T(8,128)(2,1)} %pts_ref.1, f32[8192,256]{1,0:T(8,128)} %mu_ref.1, f32[4,1,2048]{2,1,0:T(1,128)} %bitcast.3), custom_call_target="tpu_custom_call" | custom-call | tf_op jit(solution)/shard_map/pallas_call | solution.py:360
  101.8 0.0 copy-start
  101.8 0.0 copy-start.1
  101.9 7.3 %copy.10 = f32[8192,256]{1,0:T(8,128)} copy(f32[8192,256]{1,0:T(8,128)} %get-tuple-element.12) | data formatting | bytes 16777216
  109.2 0.0 copy-done
  109.2 0.6 copy.11
  109.8 0.0 copy-done.1
  109.8 0.6 copy.12
Async XLA Ops:
  101.8 7.3 %copy-start = (f32[4,1,2048]{2,1,0:T(1,128)S(1)}, f32[4,1,2048]{2,1,0:T(1,128)}, u32[]{:S(2)}) copy-start(f32[4,1,2048]{2,1,0:T(1,128)} %get-tuple-element.7) | copy-start | bytes 98308
  101.8 8.0 %copy-start.1 = (f32[1,1024]{1,0:T(1,128)S(1)}, f32[1,1024]{1,0:T(1,128)}, u32[]{:S(2)}) copy-start(f32[1,1024]{1,0:T(1,128)} %get-tuple-element.8) | copy-start | bytes 12292

commit v3 on v2

v3 whole, which is shorter than its diff:
```python
import functools
import math

import jax
import jax.numpy as jnp
from jax import lax
from jax.experimental import pallas as pl
from jax.experimental.pallas import tpu as pltpu
from jax.sharding import PartitionSpec as P

EPS_COUNT = 1e-6
ALPHA = 1e-3
LOG2E = math.log2(math.e)
LN2 = math.log(2.0)
KB = 512
IB = 256
KT = 64
MB = 1024
EARLY = 3
FB = 256
MESH = pl.DeviceIdType.MESH
F32 = jnp.float32
BF16 = jnp.bfloat16
NT = (((1,), (1,)), ((), ()))


def fit_kernel(cfg, temp_ref, pts_ref, mu_ref, logpi_ref, means_ref, logw_ref, lse_out_ref,
               x_ref, p_ref, mub_ref, muf_ref, c_ref, crow_ref, cfrow_ref, s_ref, n_ref,
               m_ref, sum_ref, lse_ref, g_ref,
               loc_sem, pts_send, pts_recv, st_send, st_recv, mu_send, mu_recv,
               out_send, out_recv, w_send, w_recv):
    sweeps, own, nq, dim, norm_const = cfg
    n_kb = own // KB
    n_kt = own // KT
    n_mb = own // MB
    n_fb = own // FB
    n_ch = nq // IB
    fit = lax.axis_index("fit")
    comp = lax.axis_index("comp")
    data = lax.axis_index("data")
    xpos = data // 2

    def data_xor(d):
        if d == 0:
            return data
        if d == 1:
            return data + 1 - 2 * (data % 2)
        if d == 2:
            return (data + 2) % 4
        return (data + 1 - 2 * (data % 2) + 2) % 4

    def peer(r):
        return (fit, (comp + r // 4) % 2, data_xor(r % 4))

    sib, par = data_xor(1), data_xor(2)
    me = comp * 4 + data

    barrier = pltpu.get_barrier_semaphore()
    for r in range(1, 8):
        pl.semaphore_signal(barrier, inc=1, device_id=peer(r), device_id_type=MESH)

    ld_pts = pltpu.make_async_copy(pts_ref, x_ref.at[pl.ds(pl.multiple_of(data * nq, nq), nq)], loc_sem.at[0])
    ld_mu = pltpu.make_async_copy(mu_ref.at[pl.ds(pl.multiple_of(data * own, own), own)], s_ref, loc_sem.at[1])
    ld_pi = pltpu.make_async_copy(logpi_ref.at[data], crow_ref, loc_sem.at[2])
    ld_pts.start()
    ld_mu.start()
    ld_pi.start()
    pl.semaphore_wait(barrier, 7)

    def pts_copy(kind, ch):
        owner = data if kind < 2 else par
        rows = pl.ds(pl.multiple_of(owner * nq + ch * IB, IB), IB)
        src = pts_ref.at[pl.ds(ch * IB, IB)] if kind < 2 else x_ref.at[rows]
        dev = peer(2) if kind == 1 else peer(1)
        return pltpu.make_async_remote_copy(
            src_ref=src, dst_ref=x_ref.at[rows], send_sem=pts_send.at[kind, ch], recv_sem=pts_recv.at[kind, ch],
            device_id=dev, device_id_type=MESH)

    for ch in range(n_ch):
        pts_copy(1, ch).start()
    for ch in range(n_ch):
        pts_copy(0, ch).start()

    def to_col(row):
        return jnp.transpose(jnp.broadcast_to(row, (128, row.shape[1])))

    def to_row(col):
        return jnp.transpose(col)[0:1, :]

    ld_pi.wait()
    ld_mu.wait()
    beta0 = temp_ref[0]

    def init_body(kb, _):
        rows = pl.ds(pl.multiple_of(kb * KB, KB), KB)
        mu = s_ref[rows, :]
        mub_ref[rows, :] = mu.astype(BF16)
        msq = jnp.sum(mu * mu, axis=1, keepdims=True)
        lp = to_col(crow_ref[:, rows])
        c_ref[rows, :] = LOG2E * (lp - beta0 * msq)
        return 0

    lax.fori_loop(0, n_kb, init_body, 0)

    def e_tile(i0, tb):
        cols = pl.ds(pl.multiple_of(i0, IB), IB)
        xt = x_ref[cols, :]
        for kb in range(n_kb):
            a = lax.dot_general(mub_ref[pl.ds(kb * KB, KB), :], xt, NT, preferred_element_type=F32)
            for u in range(KB // KT):
                rows = pl.ds(kb * KB + u * KT, KT)
                tile = kb * (KB // KT) + u
                cc = c_ref[rows, :]
                l = a[u * KT:(u + 1) * KT, :] * tb + jnp.concatenate([cc, cc], axis=1)
                l3 = l.reshape(KT // 8, 8, IB)
                m = jnp.max(l3, axis=0)
                p3 = jnp.exp2(l3 - m[None])
                p_ref[rows, cols] = p3.reshape(KT, IB)
                m_ref[tile, :, cols] = m
                sum_ref[tile, :, cols] = jnp.sum(p3, axis=0)

    def e_quarter(q, tb):
        for it in range(n_ch):
            e_tile(q * nq + it * IB, tb)

    def st_copy(t, q, r):
        return pltpu.make_async_remote_copy(
            src_ref=g_ref.at[t, q, me], dst_ref=g_ref.at[t, q, me], send_sem=st_send.at[t, q, r],
            recv_sem=st_recv.at[t, q, r], device_id=peer(r), device_id_type=MESH)

    def st_send_all(t, q):
        cols = pl.ds(pl.multiple_of(q * nq, nq), nq)
        top = jnp.max(jnp.max(m_ref[:, :, cols], axis=0), axis=0, keepdims=True)
        part = [pl.ds(k, 8) for k in range(0, n_kt, 8)]
        tot = functools.reduce(lambda u, v: u + v,
                               [jnp.sum(sum_ref[k, :, cols] * jnp.exp2(m_ref[k, :, cols] - top), axis=0) for k in part])
        tot = jnp.sum(tot, axis=0, keepdims=True)
        g_ref[t, q, me] = top + LOG2E * jnp.log(tot)
        for r in range(1, 8):
            st_copy(t, q, r).start()

    def e_step(t, q, tb):
        e_quarter(q, tb)
        st_send_all(t, q)

    def st_combine(t, q):
        for r in range(1, 8):
            st_copy(t, q, r).wait_recv()
        cols = pl.ds(pl.multiple_of(q * nq, nq), nq)
        vals = g_ref[t, q]
        top = jnp.max(vals, axis=0)
        tot = jnp.sum(jnp.exp2(vals - top[None]), axis=0)
        lse = top + LOG2E * jnp.log(tot)
        lse_ref[:, cols] = lse
        m_ref[:, :, cols] = jnp.exp2(m_ref[:, :, cols] - lse)

    def m_block(kb, quarters):
        rows = pl.ds(pl.multiple_of(kb * MB, MB), MB)
        n_acc = jnp.zeros((MB, 128), F32)
        acc = jnp.zeros((MB, dim), F32)
        for q in quarters:
            for ic in range(n_ch):
                cols = pl.ds(q * nq + ic * IB, IB)
                sc = m_ref[pl.ds(kb * (MB // KT), MB // KT), :, cols]
                r = (p_ref[rows, cols].reshape(MB // KT, KT // 8, 8, IB) * sc[:, None]).reshape(MB, IB)
                n_acc = n_acc + (r[:, :128] + r[:, 128:])
                acc = acc + jnp.dot(r.astype(BF16), x_ref[cols, :], preferred_element_type=F32)
        return n_acc, acc

    def m_first(kb, _):
        rows = pl.ds(pl.multiple_of(kb * MB, MB), MB)
        n_acc, acc = m_block(kb, (0, 2))
        n_ref[rows, :] = n_acc
        s_ref[rows, :] = acc
        return 0

    def finish(n_acc, acc):
        n = jnp.sum(n_acc, axis=1, keepdims=True)
        mu = acc * (1.0 / (n + EPS_COUNT))
        return n, mu

    def mu_copy(j):
        rows = pl.ds(pl.multiple_of(j * FB, FB), FB)
        return pltpu.make_async_remote_copy(
            src_ref=mub_ref.at[rows], dst_ref=muf_ref.at[rows], send_sem=mu_send.at[j], recv_sem=mu_recv.at[j],
            device_id=peer(2), device_id_type=MESH)

    def c_copy():
        return pltpu.make_async_remote_copy(
            src_ref=crow_ref, dst_ref=cfrow_ref, send_sem=mu_send.at[n_fb], recv_sem=mu_recv.at[n_fb],
            device_id=peer(2), device_id_type=MESH)

    def m_second(kb, beta_next, share):
        rows = pl.ds(pl.multiple_of(kb * MB, MB), MB)
        n_acc, acc = m_block(kb, (1, 3))
        n, mu = finish(n_ref[rows, :] + n_acc, s_ref[rows, :] + acc)
        mub_ref[rows, :] = mu.astype(BF16)
        msq = jnp.sum(mu * mu, axis=1, keepdims=True)
        lp = jnp.log((jnp.broadcast_to(n, (MB, 128)) + ALPHA) / norm_const)
        c = LOG2E * (lp - beta_next * msq)
        c_ref[rows, :] = c
        if share:
            crow_ref[:, rows] = to_row(c)

    def out_copy(slot, kb):
        size = (MB, FB)[slot]
        owner = data if slot == 0 else par
        rows = pl.ds(pl.multiple_of(owner * own + kb * size, size), size)
        return pltpu.make_async_remote_copy(
            src_ref=means_ref.at[rows], dst_ref=means_ref.at[rows], send_sem=out_send.at[slot, kb],
            recv_sem=out_recv.at[slot, kb], device_id=peer(1), device_id_type=MESH)

    def w_copy(slot):
        owner = data if slot == 0 else par
        return pltpu.make_async_remote_copy(
            src_ref=logw_ref.at[owner], dst_ref=logw_ref.at[owner], send_sem=w_send.at[slot], recv_sem=w_recv.at[slot],
            device_id=peer(1), device_id_type=MESH)

    def emit(slot, kb, n_acc, acc):
        size = (MB, FB)[slot]
        owner = data if slot == 0 else par
        n, mu = finish(n_acc, acc)
        means_ref[pl.ds(pl.multiple_of(owner * own + kb * size, size), size), :] = mu
        nrow = to_row(jnp.broadcast_to(n, (size, 128)))
        logw_ref[owner, :, pl.ds(pl.multiple_of(kb * size, size), size)] = jnp.log((nrow + ALPHA) / norm_const)
        out_copy(slot, kb).start()

    for t in range(sweeps):
        beta = temp_ref[t]
        tb = (2.0 * LOG2E) * beta
        last = t == sweeps - 1
        if t == 0:
            ld_pts.wait()
            for ch in range(n_ch):
                pts_copy(0, ch).wait_recv()
            lax.fori_loop(0, 2, lambda s, _: (e_step(0, xpos * 2 + s, tb), 0)[1], 0)

            def far_points(ch, _):
                pts_copy(1, ch).wait_recv()
                pts_copy(2, ch).start()
                e_tile(par * nq + ch * IB, tb)
                pts_copy(2, ch).wait_recv()
                e_tile(data_xor(3) * nq + ch * IB, tb)
                return 0

            lax.fori_loop(0, n_ch, far_points, 0)
            st_send_all(0, par)
            st_send_all(0, data_xor(3))
        else:
            lax.fori_loop(0, 4, lambda s, _: (e_step(t, (s % 2) * 2 + s // 2, tb), 0)[1], 0)
            if last:
                for j in range(EARLY, n_fb):
                    mu_copy(j).start()
        st_combine(t, 0)
        st_combine(t, 2)
        lax.fori_loop(0, n_mb, m_first, 0)
        st_combine(t, 1)
        st_combine(t, 3)
        if not last:
            beta_next = temp_ref[t + 1]
            share = t == sweeps - 2
            lax.fori_loop(0, n_mb, lambda kb, _: (m_second(kb, beta_next, share), 0)[1], 0)
            if share:
                c_copy().start()
                for j in range(EARLY):
                    mu_copy(j).start()
        else:
            def m_last(kb, _):
                rows = pl.ds(pl.multiple_of(kb * MB, MB), MB)
                n_acc, acc = m_block(kb, (1, 3))
                emit(0, kb, n_ref[rows, :] + n_acc, s_ref[rows, :] + acc)
                return 0

            lax.fori_loop(0, n_mb, m_last, 0)
            w_copy(0).start()
            c_copy().wait_recv()

            def far_block(kb, _):
                mu_copy(kb).wait_recv()
                rows = pl.ds(pl.multiple_of(kb * FB, FB), FB)
                c = to_col(cfrow_ref[:, rows])
                c2 = jnp.concatenate([c, c], axis=1)
                n_acc = jnp.zeros((FB, 128), F32)
                acc = jnp.zeros((FB, dim), F32)
                for ic in range(4 * n_ch):
                    cols = pl.ds(ic * IB, IB)
                    xt = x_ref[cols, :]
                    a = lax.dot_general(muf_ref[rows, :], xt, NT, preferred_element_type=F32)
                    r = jnp.exp2((a * tb + c2) - lse_ref[:, cols])
                    n_acc = n_acc + (r[:, :128] + r[:, 128:])
                    acc = acc + jnp.dot(r.astype(BF16), xt, preferred_element_type=F32)
                emit(1, kb, n_acc, acc)
                return 0

            lax.fori_loop(0, n_fb, far_block, 0)
            w_copy(1).start()
            mine = pl.ds(pl.multiple_of(data * nq, nq), nq)
            xo = x_ref[mine, :].astype(F32)
            sq = xo * xo
            hi = sq.astype(BF16)
            lo = (sq - hi.astype(F32)).astype(BF16)
            ones = jnp.ones((8, dim), BF16)
            row_sq = (lax.dot_general(ones, hi, NT, preferred_element_type=F32)
                      + lax.dot_general(ones, lo, NT, preferred_element_type=F32))
            lse_out_ref[...] = LN2 * lse_ref[:, mine] - beta * row_sq[0:1, :]

    for kind in range(3):
        for ch in range(n_ch):
            pts_copy(kind, ch).wait_send()
    for t in range(sweeps):
        for q in range(4):
            for r in range(1, 8):
                st_copy(t, q, r).wait_send()
    for j in range(n_fb):
        mu_copy(j).wait_send()
    c_copy().wait_send()
    for slot in range(2):
        w_copy(slot).wait_send()
        for kb in range((n_mb, n_fb)[slot]):
            out_copy(slot, kb).wait_send()

    def sibling(dev_slot):
        owner = (sib, data_xor(3))[dev_slot]
        size = (MB, FB)[dev_slot]
        for kb in range((n_mb, n_fb)[dev_slot]):
            rows = pl.ds(pl.multiple_of(owner * own + kb * size, size), size)
            pltpu.make_async_remote_copy(
                src_ref=means_ref.at[rows], dst_ref=means_ref.at[rows], send_sem=out_send.at[dev_slot, kb],
                recv_sem=out_recv.at[dev_slot, kb], device_id=peer(1), device_id_type=MESH).wait_recv()
        pltpu.make_async_remote_copy(
            src_ref=logw_ref.at[owner], dst_ref=logw_ref.at[owner], send_sem=w_send.at[dev_slot],
            recv_sem=w_recv.at[dev_slot], device_id=peer(1), device_id_type=MESH).wait_recv()

    sibling(0)
    sibling(1)


def solution(mesh):
    comp_size = mesh.shape["comp"]
    data_size = mesh.shape["data"]

    def local_fit(points, mu_init, logpi_init, inv_temp):
        nq, dim = points.shape
        rows = mu_init.shape[0]
        own = rows // data_size
        sweeps = inv_temp.shape[0]
        n_pts = nq * data_size
        n_kb = own // KB
        norm_const = n_pts + rows * comp_size * ALPHA
        cfg = (sweeps, own, nq, dim, norm_const)
        any_spec = pl.BlockSpec(memory_space=pl.ANY)
        vmem_spec = pl.BlockSpec(memory_space=pltpu.VMEM)
        dma = pltpu.SemaphoreType.DMA
        n_fb = own // FB
        means, logw, lse = pl.pallas_call(
            functools.partial(fit_kernel, cfg),
            out_shape=(pltpu.VMEM((rows, dim), F32),
                       pltpu.VMEM((data_size, 1, own), F32),
                       pltpu.VMEM((1, nq), F32)),
            in_specs=[pl.BlockSpec(memory_space=pltpu.SMEM), any_spec, any_spec, any_spec],
            out_specs=(vmem_spec, vmem_spec, vmem_spec),
            scratch_shapes=[
                pltpu.VMEM((n_pts, dim), BF16),
                pltpu.VMEM((own, n_pts), F32),
                pltpu.VMEM((own, dim), BF16),
                pltpu.VMEM((own, dim), BF16),
                pltpu.VMEM((own, 128), F32),
                pltpu.VMEM((1, own), F32),
                pltpu.VMEM((1, own), F32),
                pltpu.VMEM((own, dim), F32),
                pltpu.VMEM((own, 128), F32),
                pltpu.VMEM((own // KT, 8, n_pts), F32),
                pltpu.VMEM((own // KT, 8, n_pts), F32),
                pltpu.VMEM((1, n_pts), F32),
                pltpu.VMEM((sweeps, data_size, 8, 1, nq), F32),
                dma((3,)),
                dma((3, nq // IB)), dma((3, nq // IB)),
                dma((sweeps, 4, 8)), dma((sweeps, 4, 8)),
                dma((n_fb + 1,)), dma((n_fb + 1,)),
                dma((2, n_fb)), dma((2, n_fb)),
                dma((2,)), dma((2,)),
            ],
            compiler_params=pltpu.CompilerParams(
                collective_id=0, has_side_effects=True, vmem_limit_bytes=54 * 1024 * 1024),
        )(inv_temp, points, mu_init, logpi_init.reshape(data_size, 1, own))
        return means, logw.reshape(rows), lse.reshape(nq)

    row_spec = P(("fit", "data"), None)
    comp_spec = P(("fit", "comp"), None)
    weight_spec = P(("fit", "comp"))
    lse_spec = P(("fit", "data"))
    return jax.shard_map(local_fit, mesh=mesh, in_specs=(row_spec, comp_spec, weight_spec, P(None)), out_specs=(comp_spec, weight_spec, lse_spec), check_vma=False)
```

time: 111 us -> 86.8 us (0.78)
  Pallas kernels: 101 us -> 81.4 us
  local copies, waits for them, and re-layouts: 8.54 us -> 4.61 us
    pallas_call x1, Pallas kernels: 101 us -> 81.4 us  [local_fit(): pl.pallas_call(functools.partial(fit_kernel, cfg), out_shape=(pltpu.VMEM(...]
    unnamed x7 -> x3, local copies, waits for them, and re-layouts: 8.54 us -> 4.61 us
where the time goes in v3:
time: 86.8 us; the launch traced here: 86.7 us
  Pallas kernels  81.4 us (94%)
  local copies, waits for them, and re-layouts  4.61 us (5%)
    pallas_call x1, Pallas kernels, local_fit(): pl.pallas_call(functools.partial(fit_kernel, cfg), out_shape=(pltpu.VMEM(...  81.4 us
    unnamed x3, local copies, waits for them, and re-layouts  4.61 us

profile of v3, /device:TPU:0, one launch (start us, length us, event | category | flops | bytes accessed | tf_op | source)
XLA Modules:
  0.0 86.7 jit_solution(9185258789800412479)
XLA Ops:
  0.6 81.4 %shard_map.67 = (f32[8192,256]{1,0:T(8,128)S(1)}, f32[4,1,2048]{2,1,0:T(1,128)S(1)}, f32[1,1024]{1,0:T(1,128)S(1)}) custom-call(f32[3]{0:T(128)} %temp_ref.1, bf16[1024,256]{1,0:T(8,128)(2,1)} %pts_ref.1, f32[8192,256]{1,0:T(8,128)} %mu_ref.1, f32[4,1,2048]{2,1,0:T(1,128)} %bitcast.5), custom_call_target="tpu_custom_call" | custom-call | tf_op jit(solution)/shard_map/pallas_call | solution.py:355
  82.1 3.4 %copy.10 = f32[8192,256]{1,0:T(8,128)} copy(f32[8192,256]{1,0:T(8,128)S(1)} %get-tuple-element.9) | data formatting | bytes 16777216
  85.5 0.6 copy.11
  86.1 0.6 copy.12

commit v4 on v3

--- a/solution.py
+++ b/solution.py
@@ -10,6 +10,7 @@
 
 EPS_COUNT = 1e-6
 ALPHA = 1e-3
+PIECES = 8
 LOG2E = math.log2(math.e)
 LN2 = math.log(2.0)
 KB = 512
@@ -27,7 +28,7 @@
 def fit_kernel(cfg, temp_ref, pts_ref, mu_ref, logpi_ref, means_ref, logw_ref, lse_out_ref,
                x_ref, p_ref, mub_ref, muf_ref, c_ref, crow_ref, cfrow_ref, s_ref, n_ref,
                m_ref, sum_ref, lse_ref, g_ref,
-               loc_sem, pts_send, pts_recv, st_send, st_recv, mu_send, mu_recv,
+               loc_sem, q_sem, sib_send, pts_send, pts_recv, st_send, st_recv, mu_send, mu_recv,
                out_send, out_recv, w_send, w_recv):
     sweeps, own, nq, dim, norm_const = cfg
     n_kb = own // KB
@@ -59,27 +60,39 @@
     for r in range(1, 8):
         pl.semaphore_signal(barrier, inc=1, device_id=peer(r), device_id_type=MESH)
 
-    ld_pts = pltpu.make_async_copy(pts_ref, x_ref.at[pl.ds(pl.multiple_of(data * nq, nq), nq)], loc_sem.at[0])
-    ld_mu = pltpu.make_async_copy(mu_ref.at[pl.ds(pl.multiple_of(data * own, own), own)], s_ref, loc_sem.at[1])
-    ld_pi = pltpu.make_async_copy(logpi_ref.at[data], crow_ref, loc_sem.at[2])
+    def blk(i, size):
+        return pl.ds(pl.multiple_of(i * size, size), size)
+
+    ld_pts = pltpu.make_async_copy(pts_ref, x_ref.at[blk(data, nq)], q_sem.at[0])
+    ld_mu = [pltpu.make_async_copy(mu_ref.at[blk(o, own)], means_ref.at[blk(o, own)], loc_sem.at[i])
+             for i, o in enumerate((data, par))]
+    ld_pi = [pltpu.make_async_copy(logpi_ref.at[o], dst, loc_sem.at[2 + i])
+             for i, (o, dst) in enumerate(((data, crow_ref), (par, cfrow_ref)))]
     ld_pts.start()
-    ld_mu.start()
-    ld_pi.start()
+    for cp in ld_mu + ld_pi:
+        cp.start()
     pl.semaphore_wait(barrier, 7)
 
+    def sib_copy():
+        return pltpu.make_async_remote_copy(
+            src_ref=pts_ref, dst_ref=x_ref.at[blk(data, nq)], send_sem=sib_send, recv_sem=q_sem.at[1],
+            device_id=peer(1), device_id_type=MESH)
+
     def pts_copy(kind, ch):
-        owner = data if kind < 2 else par
-        rows = pl.ds(pl.multiple_of(owner * nq + ch * IB, IB), IB)
-        src = pts_ref.at[pl.ds(ch * IB, IB)] if kind < 2 else x_ref.at[rows]
-        dev = peer(2) if kind == 1 else peer(1)
-        return pltpu.make_async_remote_copy(
-            src_ref=src, dst_ref=x_ref.at[rows], send_sem=pts_send.at[kind, ch], recv_sem=pts_recv.at[kind, ch],
-            device_id=dev, device_id_type=MESH)
-
-    for ch in range(n_ch):
+        owner = (data, par)[kind]
+        rows = blk(owner * n_ch + ch, IB)
+        return pltpu.make_async_remote_copy(
+            src_ref=pts_ref.at[pl.ds(ch * IB, IB)] if kind == 0 else x_ref.at[rows], dst_ref=x_ref.at[rows],
+            send_sem=pts_send.at[kind, ch], recv_sem=pts_recv.at[kind, ch],
+            device_id=peer(2 - kind), device_id_type=MESH)
+
+    def pass_on(ch):
+        pts_copy(0, ch).wait_recv()
         pts_copy(1, ch).start()
+
     for ch in range(n_ch):
         pts_copy(0, ch).start()
+    sib_copy().start()
 
     def to_col(row):
         return jnp.transpose(jnp.broadcast_to(row, (128, row.shape[1])))
@@ -87,53 +100,56 @@
     def to_row(col):
         return jnp.transpose(col)[0:1, :]
 
-    ld_pi.wait()
-    ld_mu.wait()
     beta0 = temp_ref[0]
-
-    def init_body(kb, _):
-        rows = pl.ds(pl.multiple_of(kb * KB, KB), KB)
-        mu = s_ref[rows, :]
-        mub_ref[rows, :] = mu.astype(BF16)
-        msq = jnp.sum(mu * mu, axis=1, keepdims=True)
-        lp = to_col(crow_ref[:, rows])
-        c_ref[rows, :] = LOG2E * (lp - beta0 * msq)
-        return 0
-
-    lax.fori_loop(0, n_kb, init_body, 0)
-
-    def e_tile(i0, tb):
+    for i, (o, low, row, col) in enumerate(((data, mub_ref, crow_ref, c_ref), (par, muf_ref, cfrow_ref, n_ref))):
+        ld_mu[i].wait()
+        ld_pi[i].wait()
+
+        def init_body(kb, _, o=o, low=low, row=row, col=col):
+            rows = blk(kb, KB)
+            mu = means_ref[blk(o * n_kb + kb, KB), :]
+            low[rows, :] = mu.astype(BF16)
+            msq = jnp.sum(mu * mu, axis=1, keepdims=True)
+            col[rows, :] = LOG2E * (to_col(row[:, rows]) - beta0 * msq)
+            return 0
+
+        lax.fori_loop(0, n_kb, init_body, 0)
+
+    def e_tile(i0, tb, low, col, s0, keep):
         cols = pl.ds(pl.multiple_of(i0, IB), IB)
+        scols = pl.ds(pl.multiple_of(s0, IB), IB)
         xt = x_ref[cols, :]
         for kb in range(n_kb):
-            a = lax.dot_general(mub_ref[pl.ds(kb * KB, KB), :], xt, NT, preferred_element_type=F32)
+            a = lax.dot_general(low[pl.ds(kb * KB, KB), :], xt, NT, preferred_element_type=F32)
             for u in range(KB // KT):
                 rows = pl.ds(kb * KB + u * KT, KT)
                 tile = kb * (KB // KT) + u
-                cc = c_ref[rows, :]
+                cc = col[rows, :]
                 l = a[u * KT:(u + 1) * KT, :] * tb + jnp.concatenate([cc, cc], axis=1)
                 l3 = l.reshape(KT // 8, 8, IB)
                 m = jnp.max(l3, axis=0)
                 p3 = jnp.exp2(l3 - m[None])
-                p_ref[rows, cols] = p3.reshape(KT, IB)
-                m_ref[tile, :, cols] = m
-                sum_ref[tile, :, cols] = jnp.sum(p3, axis=0)
-
-    def e_quarter(q, tb):
+                if keep:
+                    p_ref[rows, cols] = p3.reshape(KT, IB)
+                m_ref[tile, :, scols] = m
+                sum_ref[tile, :, scols] = jnp.sum(p3, axis=0)
+
+    def e_quarter(q, tb, low=mub_ref, col=c_ref, sq=None, keep=True):
         for it in range(n_ch):
-            e_tile(q * nq + it * IB, tb)
+            e_tile(q * nq + it * IB, tb, low, col, (q if sq is None else sq) * nq + it * IB, keep)
 
     def st_copy(t, q, r):
         return pltpu.make_async_remote_copy(
             src_ref=g_ref.at[t, q, me], dst_ref=g_ref.at[t, q, me], send_sem=st_send.at[t, q, r],
             recv_sem=st_recv.at[t, q, r], device_id=peer(r), device_id_type=MESH)
 
-    def st_send_all(t, q):
-        cols = pl.ds(pl.multiple_of(q * nq, nq), nq)
-        top = jnp.max(jnp.max(m_ref[:, :, cols], axis=0), axis=0, keepdims=True)
-        part = [pl.ds(k, 8) for k in range(0, n_kt, 8)]
+    def st_send_all(t, q, stats):
+        cols = [blk(c, nq) for c in stats]
+        top = functools.reduce(jnp.maximum, [jnp.max(m_ref[:, :, c], axis=0) for c in cols])
+        top = jnp.max(top, axis=0, keepdims=True)
         tot = functools.reduce(lambda u, v: u + v,
-                               [jnp.sum(sum_ref[k, :, cols] * jnp.exp2(m_ref[k, :, cols] - top), axis=0) for k in part])
+                               [jnp.sum(sum_ref[pl.ds(k, 8), :, c] * jnp.exp2(m_ref[pl.ds(k, 8), :, c] - top), axis=0)
+                                for c in cols for k in range(0, n_kt, 8)])
         tot = jnp.sum(tot, axis=0, keepdims=True)
         g_ref[t, q, me] = top + LOG2E * jnp.log(tot)
         for r in range(1, 8):
@@ -141,18 +157,28 @@
 
     def e_step(t, q, tb):
         e_quarter(q, tb)
-        st_send_all(t, q)
+        st_send_all(t, q, (q,))
+
+    def combine(q, vals):
+        top = functools.reduce(jnp.maximum, [jnp.max(v, axis=0) for v in vals])
+        tot = functools.reduce(lambda u, v: u + v, [jnp.sum(jnp.exp2(v - top[None]), axis=0) for v in vals])
+        lse = top + LOG2E * jnp.log(tot)
+        lse_ref[:, blk(q, nq)] = lse
+        return lse
+
+    def scale(q, lse):
+        cols = blk(q, nq)
+        m_ref[:, :, cols] = jnp.exp2(m_ref[:, :, cols] - lse)
 
     def st_combine(t, q):
         for r in range(1, 8):
             st_copy(t, q, r).wait_recv()
-        cols = pl.ds(pl.multiple_of(q * nq, nq), nq)
-        vals = g_ref[t, q]
-        top = jnp.max(vals, axis=0)
-        tot = jnp.sum(jnp.exp2(vals - top[None]), axis=0)
-        lse = top + LOG2E * jnp.log(tot)
-        lse_ref[:, cols] = lse
-        m_ref[:, :, cols] = jnp.exp2(m_ref[:, :, cols] - lse)
+        scale(q, combine(q, [g_ref[t, q]]))
+
+    def st_combine_four(q, x, rs):
+        for r in rs:
+            st_copy(0, q, r).wait_recv()
+        return combine(q, [g_ref[0, q, pl.ds(4 * c + 2 * x, 2)] for c in range(2)])
 
     def m_block(kb, quarters):
         rows = pl.ds(pl.multiple_of(kb * MB, MB), MB)
@@ -160,19 +186,32 @@
         acc = jnp.zeros((MB, dim), F32)
         for q in quarters:
             for ic in range(n_ch):
-                cols = pl.ds(q * nq + ic * IB, IB)
+                cols = blk(q * n_ch + ic, IB)
                 sc = m_ref[pl.ds(kb * (MB // KT), MB // KT), :, cols]
                 r = (p_ref[rows, cols].reshape(MB // KT, KT // 8, 8, IB) * sc[:, None]).reshape(MB, IB)
                 n_acc = n_acc + (r[:, :128] + r[:, 128:])
                 acc = acc + jnp.dot(r.astype(BF16), x_ref[cols, :], preferred_element_type=F32)
         return n_acc, acc
 
-    def m_first(kb, _):
-        rows = pl.ds(pl.multiple_of(kb * MB, MB), MB)
-        n_acc, acc = m_block(kb, (0, 2))
+    def m_first(kb, quarters):
+        rows = blk(kb, MB)
+        n_acc, acc = m_block(kb, quarters)
         n_ref[rows, :] = n_acc
         s_ref[rows, :] = acc
         return 0
+
+    def flash(low, rows, c, tb, chunks, size):
+        c2 = jnp.concatenate([c, c], axis=1)
+        n_acc = jnp.zeros((size, 128), F32)
+        acc = jnp.zeros((size, dim), F32)
+        for ch in chunks:
+            cols = blk(ch, IB)
+            xt = x_ref[cols, :]
+            a = lax.dot_general(low[rows, :], xt, NT, preferred_element_type=F32)
+            r = jnp.exp2((a * tb + c2) - lse_ref[:, cols])
+            n_acc = n_acc + (r[:, :128] + r[:, 128:])
+            acc = acc + jnp.dot(r.astype(BF16), xt, preferred_element_type=F32)
+        return n_acc, acc
 
     def finish(n_acc, acc):
         n = jnp.sum(n_acc, axis=1, keepdims=True)
@@ -190,17 +229,16 @@
             src_ref=crow_ref, dst_ref=cfrow_ref, send_sem=mu_send.at[n_fb], recv_sem=mu_recv.at[n_fb],
             device_id=peer(2), device_id_type=MESH)
 
-    def m_second(kb, beta_next, share):
-        rows = pl.ds(pl.multiple_of(kb * MB, MB), MB)
-        n_acc, acc = m_block(kb, (1, 3))
+    def renew(rows, size, n_acc, acc, beta_next, share):
         n, mu = finish(n_ref[rows, :] + n_acc, s_ref[rows, :] + acc)
         mub_ref[rows, :] = mu.astype(BF16)
         msq = jnp.sum(mu * mu, axis=1, keepdims=True)
-        lp = jnp.log((jnp.broadcast_to(n, (MB, 128)) + ALPHA) / norm_const)
+        lp = jnp.log((jnp.broadcast_to(n, (size, 128)) + ALPHA) / norm_const)
         c = LOG2E * (lp - beta_next * msq)
         c_ref[rows, :] = c
         if share:
             crow_ref[:, rows] = to_row(c)
+        return 0
 
     def out_copy(slot, kb):
         size = (MB, FB)[slot]
@@ -230,36 +268,52 @@
         tb = (2.0 * LOG2E) * beta
         last = t == sweeps - 1
         if t == 0:
-            ld_pts.wait()
+            def own_points(s, _):
+                q = data + s * (sib - data)
+                pltpu.make_async_copy(pts_ref, x_ref.at[blk(q, nq)], q_sem.at[s]).wait()
+                far = (q + 2) % 4
+                e_quarter(q, tb)
+                e_quarter(q, tb, muf_ref, n_ref, far, False)
+                st_send_all(0, q, (q, far))
+                return 0
+
+            lax.fori_loop(0, 2, own_points, 0)
+            pass_on(0)
+            pass_on(1)
+            near = (xpos * 2, xpos * 2 + 1)
+            away = ((1 - xpos) * 2, (1 - xpos) * 2 + 1)
+            for q in near:
+                scale(q, st_combine_four(q, xpos, (1, 4, 5)))
+            lax.fori_loop(0, n_mb, lambda kb, _: m_first(kb, near), 0)
+            pass_on(2)
+            pass_on(3)
+            for q in away:
+                st_combine_four(q, 1 - xpos, (2, 3, 6, 7))
             for ch in range(n_ch):
-                pts_copy(0, ch).wait_recv()
-            lax.fori_loop(0, 2, lambda s, _: (e_step(0, xpos * 2 + s, tb), 0)[1], 0)
-
-            def far_points(ch, _):
                 pts_copy(1, ch).wait_recv()
-                pts_copy(2, ch).start()
-                e_tile(par * nq + ch * IB, tb)
-                pts_copy(2, ch).wait_recv()
-                e_tile(data_xor(3) * nq + ch * IB, tb)
-                return 0
-
-            lax.fori_loop(0, n_ch, far_points, 0)
-            st_send_all(0, par)
-            st_send_all(0, data_xor(3))
-        else:
-            lax.fori_loop(0, 4, lambda s, _: (e_step(t, (s % 2) * 2 + s // 2, tb), 0)[1], 0)
-            if last:
-                for j in range(EARLY, n_fb):
-                    mu_copy(j).start()
+            beta_next = temp_ref[1]
+            chunks = [q * n_ch + ic for q in away for ic in range(n_ch)]
+
+            def away_block(kb, _):
+                rows = blk(kb, KB)
+                n_acc, acc = flash(mub_ref, rows, c_ref[rows, :], tb, chunks, KB)
+                return renew(rows, KB, n_acc, acc, beta_next, False)
+
+            lax.fori_loop(0, n_kb, away_block, 0)
+            continue
+        lax.fori_loop(0, 4, lambda s, _: (e_step(t, (s % 2) * 2 + s // 2, tb), 0)[1], 0)
+        if last:
+            for j in range(EARLY, n_fb):
+                mu_copy(j).start()
         st_combine(t, 0)
         st_combine(t, 2)
-        lax.fori_loop(0, n_mb, m_first, 0)
+        lax.fori_loop(0, n_mb, lambda kb, _: m_first(kb, (0, 2)), 0)
         st_combine(t, 1)
         st_combine(t, 3)
         if not last:
             beta_next = temp_ref[t + 1]
             share = t == sweeps - 2
-            lax.fori_loop(0, n_mb, lambda kb, _: (m_second(kb, beta_next, share), 0)[1], 0)
+            lax.fori_loop(0, n_mb, lambda kb, _: renew(blk(kb, MB), MB, *m_block(kb, (1, 3)), beta_next, share), 0)
             if share:
                 c_copy().start()
                 for j in range(EARLY):
@@ -278,17 +332,7 @@
             def far_block(kb, _):
                 mu_copy(kb).wait_recv()
                 rows = pl.ds(pl.multiple_of(kb * FB, FB), FB)
-                c = to_col(cfrow_ref[:, rows])
-                c2 = jnp.concatenate([c, c], axis=1)
-                n_acc = jnp.zeros((FB, 128), F32)
-                acc = jnp.zeros((FB, dim), F32)
-                for ic in range(4 * n_ch):
-                    cols = pl.ds(ic * IB, IB)
-                    xt = x_ref[cols, :]
-                    a = lax.dot_general(muf_ref[rows, :], xt, NT, preferred_element_type=F32)
-                    r = jnp.exp2((a * tb + c2) - lse_ref[:, cols])
-                    n_acc = n_acc + (r[:, :128] + r[:, 128:])
-                    acc = acc + jnp.dot(r.astype(BF16), xt, preferred_element_type=F32)
+                n_acc, acc = flash(muf_ref, rows, to_col(cfrow_ref[:, rows]), tb, range(4 * n_ch), FB)
                 emit(1, kb, n_acc, acc)
                 return 0
 
@@ -304,11 +348,12 @@
                       + lax.dot_general(ones, lo, NT, preferred_element_type=F32))
             lse_out_ref[...] = LN2 * lse_ref[:, mine] - beta * row_sq[0:1, :]
 
-    for kind in range(3):
+    sib_copy().wait_send()
+    for kind in range(2):
         for ch in range(n_ch):
             pts_copy(kind, ch).wait_send()
     for t in range(sweeps):
-        for q in range(4):
+        for q in (near if t == 0 else range(4)):
             for r in range(1, 8):
                 st_copy(t, q, r).wait_send()
     for j in range(n_fb):
@@ -333,6 +378,18 @@
 
     sibling(0)
     sibling(1)
+
+
+def flush_kernel(means_ref, logw_ref, lse_ref, means_out, logw_out, lse_out, sem):
+    rows = means_ref.shape[0] // PIECES
+    copies = [pltpu.make_async_copy(means_ref.at[pl.ds(i * rows, rows)], means_out.at[pl.ds(i * rows, rows)], sem.at[i])
+              for i in range(PIECES)]
+    copies.append(pltpu.make_async_copy(logw_ref, logw_out, sem.at[PIECES]))
+    copies.append(pltpu.make_async_copy(lse_ref, lse_out, sem.at[PIECES + 1]))
+    for cp in copies:
+        cp.start()
+    for cp in copies:
+        cp.wait()
 
 
 def solution(mesh):
@@ -373,8 +430,8 @@
                 pltpu.VMEM((own // KT, 8, n_pts), F32),
                 pltpu.VMEM((1, n_pts), F32),
                 pltpu.VMEM((sweeps, data_size, 8, 1, nq), F32),
-                dma((3,)),
-                dma((3, nq // IB)), dma((3, nq // IB)),
+                dma((4,)), dma((2,)), dma,
+                dma((2, nq // IB)), dma((2, nq // IB)),
                 dma((sweeps, 4, 8)), dma((sweeps, 4, 8)),
                 dma((n_fb + 1,)), dma((n_fb + 1,)),
                 dma((2, n_fb)), dma((2, n_fb)),
@@ -383,6 +440,15 @@
             compiler_params=pltpu.CompilerParams(
                 collective_id=0, has_side_effects=True, vmem_limit_bytes=54 * 1024 * 1024),
         )(inv_temp, points, mu_init, logpi_init.reshape(data_size, 1, own))
+        results = [pltpu.with_memory_space_constraint(v, pltpu.VMEM) for v in (means, logw, lse)]
+        means, logw, lse = pl.pallas_call(
+            flush_kernel,
+            out_shape=tuple(jax.ShapeDtypeStruct(v.shape, F32) for v in results),
+            in_specs=[vmem_spec] * 3,
+            out_specs=(any_spec,) * 3,
+            scratch_shapes=[dma((PIECES + 2,))],
+            compiler_params=pltpu.CompilerParams(vmem_limit_bytes=16 * 1024 * 1024),
+        )(*results)
         return means, logw.reshape(rows), lse.reshape(nq)
 
     row_spec = P(("fit", "data"), None)

time: 86.8 us -> 87.5 us (level)
  Pallas kernels: 81.4 us -> 86.6 us
  local copies, waits for them, and re-layouts: 4.61 us -> 0 us
    unnamed x3 -> x0, local copies, waits for them, and re-layouts: 4.61 us -> none
    pallas_call x0 -> x1, Pallas kernels: none -> 3.39 us  [local_fit(): pl.pallas_call(flush_kernel, out_shape=tuple((jax.ShapeDtypeStruct(v.shap...]
    pallas_call x1, Pallas kernels: 81.4 us -> 83.2 us  [local_fit(): pl.pallas_call(functools.partial(fit_kernel, cfg), out_shape=(pltpu.VMEM(...]
where the time goes in v4:
time: 87.5 us; the launch traced here: 87.4 us
  Pallas kernels  86.6 us (99%)
    pallas_call x1, Pallas kernels, local_fit(): pl.pallas_call(functools.partial(fit_kernel, cfg), out_shape=(pltpu.VMEM(...  83.2 us
    pallas_call x1, Pallas kernels, local_fit(): pl.pallas_call(flush_kernel, out_shape=tuple((jax.ShapeDtypeStruct(v.shap...  3.39 us

profile of v4, /device:TPU:0, one launch (start us, length us, event | category | flops | bytes accessed | tf_op | source)
XLA Modules:
  0.0 87.4 jit_solution(7712456257356800948)
XLA Ops:
  0.6 83.2 %shard_map.67 = (f32[8192,256]{1,0:T(8,128)S(1)}, f32[4,1,2048]{2,1,0:T(1,128)S(1)}, f32[1,1024]{1,0:T(1,128)S(1)}) custom-call(f32[3]{0:T(128)} %temp_ref.1, bf16[1024,256]{1,0:T(8,128)(2,1)} %pts_ref.1, f32[8192,256]{1,0:T(8,128)} %mu_ref.1, f32[4,1,2048]{2,1,0:T(1,128)} %bitcast.3), custom_call_target="tpu_custom_call" | custom-call | tf_op jit(solution)/shard_map/pallas_call | solution.py:412
  83.8 3.4 %shard_map.68 = (f32[8192,256]{1,0:T(8,128)}, f32[4,1,2048]{2,1,0:T(1,128)}, f32[1,1024]{1,0:T(1,128)}) custom-call(f32[8192,256]{1,0:T(8,128)S(1)} %get-tuple-element.9.means_ref, f32[4,1,2048]{2,1,0:T(1,128)S(1)} %get-tuple-element.10.logw_ref, f32[1,1024]{1,0:T(1,128)S(1)} %get-tuple-element.11.lse_ref), custom_call_target="tpu_custom_call" | custom-call | tf_op jit(solution)/shard_map/pallas_call | solution.py:444

commit v5 on v4

--- a/solution.py
+++ b/solution.py
@@ -90,9 +90,9 @@
         pts_copy(0, ch).wait_recv()
         pts_copy(1, ch).start()
 
+    sib_copy().start()
     for ch in range(n_ch):
         pts_copy(0, ch).start()
-    sib_copy().start()
 
     def to_col(row):
         return jnp.transpose(jnp.broadcast_to(row, (128, row.shape[1])))
@@ -152,7 +152,7 @@
                                 for c in cols for k in range(0, n_kt, 8)])
         tot = jnp.sum(tot, axis=0, keepdims=True)
         g_ref[t, q, me] = top + LOG2E * jnp.log(tot)
-        for r in range(1, 8):
+        for r in ((5, 4, 1, 6, 7, 2, 3) if t == 0 else (6, 7, 2, 3, 5, 4, 1)):
             st_copy(t, q, r).start()
 
     def e_step(t, q, tb):

time: 87.5 us -> 87.6 us (level)
  no operation moved by 1% of the time
where the time goes in v5:
time: 87.6 us; the launch traced here: 87.4 us
  Pallas kernels  86.6 us (99%)
    pallas_call x1, Pallas kernels, local_fit(): pl.pallas_call(functools.partial(fit_kernel, cfg), out_shape=(pltpu.VMEM(...  83.3 us
    pallas_call x1, Pallas kernels, local_fit(): pl.pallas_call(flush_kernel, out_shape=tuple((jax.ShapeDtypeStruct(v.shap...  3.39 us

profile of v5, /device:TPU:0, one launch (start us, length us, event | category | flops | bytes accessed | tf_op | source)
XLA Modules:
  0.0 87.4 jit_solution(17389476803081447408)
XLA Ops:
  0.6 83.3 %shard_map.67 = (f32[8192,256]{1,0:T(8,128)S(1)}, f32[4,1,2048]{2,1,0:T(1,128)S(1)}, f32[1,1024]{1,0:T(1,128)S(1)}) custom-call(f32[3]{0:T(128)} %temp_ref.1, bf16[1024,256]{1,0:T(8,128)(2,1)} %pts_ref.1, f32[8192,256]{1,0:T(8,128)} %mu_ref.1, f32[4,1,2048]{2,1,0:T(1,128)} %bitcast.3), custom_call_target="tpu_custom_call" | custom-call | tf_op jit(solution)/shard_map/pallas_call | solution.py:412
  83.9 3.4 %shard_map.68 = (f32[8192,256]{1,0:T(8,128)}, f32[4,1,2048]{2,1,0:T(1,128)}, f32[1,1024]{1,0:T(1,128)}) custom-call(f32[8192,256]{1,0:T(8,128)S(1)} %get-tuple-element.9.means_ref, f32[4,1,2048]{2,1,0:T(1,128)S(1)} %get-tuple-element.10.logw_ref, f32[1,1024]{1,0:T(1,128)S(1)} %get-tuple-element.11.lse_ref), custom_call_target="tpu_custom_call" | custom-call | tf_op jit(solution)/shard_map/pallas_call | solution.py:444

commit v6 on v5

--- a/solution.py
+++ b/solution.py
@@ -13,20 +13,22 @@
 PIECES = 8
 LOG2E = math.log2(math.e)
 LN2 = math.log(2.0)
-KB = 512
+KB = 1024
 IB = 256
 KT = 64
 MB = 1024
 EARLY = 3
-FB = 256
+SB = 256
+FB = 512
 MESH = pl.DeviceIdType.MESH
 F32 = jnp.float32
 BF16 = jnp.bfloat16
+NN = (((1,), (0,)), ((), ()))
 NT = (((1,), (1,)), ((), ()))
 
 
 def fit_kernel(cfg, temp_ref, pts_ref, mu_ref, logpi_ref, means_ref, logw_ref, lse_out_ref,
-               x_ref, p_ref, mub_ref, muf_ref, c_ref, crow_ref, cfrow_ref, s_ref, n_ref,
+               x_ref, xt_ref, p_ref, mub_ref, muf_ref, c_ref, crow_ref, cfrow_ref, s_ref, n_ref,
                m_ref, sum_ref, lse_ref, g_ref,
                loc_sem, q_sem, sib_send, pts_send, pts_recv, st_send, st_recv, mu_send, mu_recv,
                out_send, out_recv, w_send, w_recv):
@@ -35,6 +37,7 @@
     n_kt = own // KT
     n_mb = own // MB
     n_fb = own // FB
+    n_sb = own // SB
     n_ch = nq // IB
     fit = lax.axis_index("fit")
     comp = lax.axis_index("comp")
@@ -115,12 +118,14 @@
 
         lax.fori_loop(0, n_kb, init_body, 0)
 
-    def e_tile(i0, tb, low, col, s0, keep):
+    def e_tile(i0, tb, low, col, s0, keep, first):
         cols = pl.ds(pl.multiple_of(i0, IB), IB)
         scols = pl.ds(pl.multiple_of(s0, IB), IB)
-        xt = x_ref[cols, :]
+        if first:
+            xt_ref[:, cols] = jnp.transpose(x_ref[cols, :])
+        xt = xt_ref[:, cols]
         for kb in range(n_kb):
-            a = lax.dot_general(low[pl.ds(kb * KB, KB), :], xt, NT, preferred_element_type=F32)
+            a = lax.dot_general(low[pl.ds(kb * KB, KB), :], xt, NN, preferred_element_type=F32)
             for u in range(KB // KT):
                 rows = pl.ds(kb * KB + u * KT, KT)
                 tile = kb * (KB // KT) + u
@@ -134,9 +139,9 @@
                 m_ref[tile, :, scols] = m
                 sum_ref[tile, :, scols] = jnp.sum(p3, axis=0)
 
-    def e_quarter(q, tb, low=mub_ref, col=c_ref, sq=None, keep=True):
+    def e_quarter(q, tb, low=mub_ref, col=c_ref, sq=None, keep=True, first=False):
         for it in range(n_ch):
-            e_tile(q * nq + it * IB, tb, low, col, (q if sq is None else sq) * nq + it * IB, keep)
+            e_tile(q * nq + it * IB, tb, low, col, (q if sq is None else sq) * nq + it * IB, keep, first)
 
     def st_copy(t, q, r):
         return pltpu.make_async_remote_copy(
@@ -206,11 +211,10 @@
         acc = jnp.zeros((size, dim), F32)
         for ch in chunks:
             cols = blk(ch, IB)
-            xt = x_ref[cols, :]
-            a = lax.dot_general(low[rows, :], xt, NT, preferred_element_type=F32)
+            a = lax.dot_general(low[rows, :], xt_ref[:, cols], NN, preferred_element_type=F32)
             r = jnp.exp2((a * tb + c2) - lse_ref[:, cols])
             n_acc = n_acc + (r[:, :128] + r[:, 128:])
-            acc = acc + jnp.dot(r.astype(BF16), xt, preferred_element_type=F32)
+            acc = acc + jnp.dot(r.astype(BF16), x_ref[cols, :], preferred_element_type=F32)
         return n_acc, acc
 
     def finish(n_acc, acc):
@@ -219,14 +223,14 @@
         return n, mu
 
     def mu_copy(j):
-        rows = pl.ds(pl.multiple_of(j * FB, FB), FB)
+        rows = pl.ds(pl.multiple_of(j * SB, SB), SB)
         return pltpu.make_async_remote_copy(
             src_ref=mub_ref.at[rows], dst_ref=muf_ref.at[rows], send_sem=mu_send.at[j], recv_sem=mu_recv.at[j],
             device_id=peer(2), device_id_type=MESH)
 
     def c_copy():
         return pltpu.make_async_remote_copy(
-            src_ref=crow_ref, dst_ref=cfrow_ref, send_sem=mu_send.at[n_fb], recv_sem=mu_recv.at[n_fb],
+            src_ref=crow_ref, dst_ref=cfrow_ref, send_sem=mu_send.at[n_sb], recv_sem=mu_recv.at[n_sb],
             device_id=peer(2), device_id_type=MESH)
 
     def renew(rows, size, n_acc, acc, beta_next, share):
@@ -272,7 +276,7 @@
                 q = data + s * (sib - data)
                 pltpu.make_async_copy(pts_ref, x_ref.at[blk(q, nq)], q_sem.at[s]).wait()
                 far = (q + 2) % 4
-                e_quarter(q, tb)
+                e_quarter(q, tb, first=True)
                 e_quarter(q, tb, muf_ref, n_ref, far, False)
                 st_send_all(0, q, (q, far))
                 return 0
@@ -291,19 +295,27 @@
                 st_combine_four(q, 1 - xpos, (2, 3, 6, 7))
             for ch in range(n_ch):
                 pts_copy(1, ch).wait_recv()
+            chunks = [q * n_ch + ic for q in away for ic in range(n_ch)]
+
             beta_next = temp_ref[1]
-            chunks = [q * n_ch + ic for q in away for ic in range(n_ch)]
+
+            def turn(ch, _):
+                cols = blk((1 - xpos) * 2 * n_ch + ch, IB)
+                xt_ref[:, cols] = jnp.transpose(x_ref[cols, :])
+                return 0
+
+            lax.fori_loop(0, 2 * n_ch, turn, 0)
 
             def away_block(kb, _):
-                rows = blk(kb, KB)
-                n_acc, acc = flash(mub_ref, rows, c_ref[rows, :], tb, chunks, KB)
-                return renew(rows, KB, n_acc, acc, beta_next, False)
-
-            lax.fori_loop(0, n_kb, away_block, 0)
+                rows = blk(kb, FB)
+                n_acc, acc = flash(mub_ref, rows, c_ref[rows, :], tb, chunks, FB)
+                return renew(rows, FB, n_acc, acc, beta_next, False)
+
+            lax.fori_loop(0, n_fb, away_block, 0)
             continue
         lax.fori_loop(0, 4, lambda s, _: (e_step(t, (s % 2) * 2 + s // 2, tb), 0)[1], 0)
         if last:
-            for j in range(EARLY, n_fb):
+            for j in range(EARLY, n_sb):
                 mu_copy(j).start()
         st_combine(t, 0)
         st_combine(t, 2)
@@ -330,7 +342,8 @@
             c_copy().wait_recv()
 
             def far_block(kb, _):
-                mu_copy(kb).wait_recv()
+                for j in range(FB // SB):
+                    mu_copy(kb * (FB // SB) + j).wait_recv()
                 rows = pl.ds(pl.multiple_of(kb * FB, FB), FB)
                 n_acc, acc = flash(muf_ref, rows, to_col(cfrow_ref[:, rows]), tb, range(4 * n_ch), FB)
                 emit(1, kb, n_acc, acc)
@@ -356,7 +369,7 @@
         for q in (near if t == 0 else range(4)):
             for r in range(1, 8):
                 st_copy(t, q, r).wait_send()
-    for j in range(n_fb):
+    for j in range(n_sb):
         mu_copy(j).wait_send()
     c_copy().wait_send()
     for slot in range(2):
@@ -408,7 +421,7 @@
         any_spec = pl.BlockSpec(memory_space=pl.ANY)
         vmem_spec = pl.BlockSpec(memory_space=pltpu.VMEM)
         dma = pltpu.SemaphoreType.DMA
-        n_fb = own // FB
+        n_fb, n_sb = own // FB, own // SB
         means, logw, lse = pl.pallas_call(
             functools.partial(fit_kernel, cfg),
             out_shape=(pltpu.VMEM((rows, dim), F32),
@@ -418,6 +431,7 @@
             out_specs=(vmem_spec, vmem_spec, vmem_spec),
             scratch_shapes=[
                 pltpu.VMEM((n_pts, dim), BF16),
+                pltpu.VMEM((dim, n_pts), BF16),
                 pltpu.VMEM((own, n_pts), F32),
                 pltpu.VMEM((own, dim), BF16),
                 pltpu.VMEM((own, dim), BF16),
@@ -433,7 +447,7 @@
                 dma((4,)), dma((2,)), dma,
                 dma((2, nq // IB)), dma((2, nq // IB)),
                 dma((sweeps, 4, 8)), dma((sweeps, 4, 8)),
-                dma((n_fb + 1,)), dma((n_fb + 1,)),
+                dma((n_sb + 1,)), dma((n_sb + 1,)),
                 dma((2, n_fb)), dma((2, n_fb)),
                 dma((2,)), dma((2,)),
             ],

time: 87.6 us -> 87.6 us (level)
  no operation moved by 1% of the time
where the time goes in v6:
time: 87.6 us; the launch traced here: 87.5 us
  Pallas kernels  86.7 us (99%)
    pallas_call x1, Pallas kernels, local_fit(): pl.pallas_call(functools.partial(fit_kernel, cfg), out_shape=(pltpu.VMEM(...  83.3 us
    pallas_call x1, Pallas kernels, local_fit(): pl.pallas_call(flush_kernel, out_shape=tuple((jax.ShapeDtypeStruct(v.shap...  3.39 us

profile of v6, /device:TPU:0, one launch (start us, length us, event | category | flops | bytes accessed | tf_op | source)
XLA Modules:
  0.0 87.5 jit_solution(13495441694213216498)
XLA Ops:
  0.6 83.3 %shard_map.67 = (f32[8192,256]{1,0:T(8,128)S(1)}, f32[4,1,2048]{2,1,0:T(1,128)S(1)}, f32[1,1024]{1,0:T(1,128)S(1)}) custom-call(f32[3]{0:T(128)} %temp_ref.1, bf16[1024,256]{1,0:T(8,128)(2,1)} %pts_ref.1, f32[8192,256]{1,0:T(8,128)} %mu_ref.1, f32[4,1,2048]{2,1,0:T(1,128)} %bitcast.3), custom_call_target="tpu_custom_call" | custom-call | tf_op jit(solution)/shard_map/pallas_call | solution.py:425
  83.9 3.4 %shard_map.68 = (f32[8192,256]{1,0:T(8,128)}, f32[4,1,2048]{2,1,0:T(1,128)}, f32[1,1024]{1,0:T(1,128)}) custom-call(f32[8192,256]{1,0:T(8,128)S(1)} %get-tuple-element.9.means_ref, f32[4,1,2048]{2,1,0:T(1,128)S(1)} %get-tuple-element.10.logw_ref, f32[1,1024]{1,0:T(1,128)S(1)} %get-tuple-element.11.lse_ref), custom_call_target="tpu_custom_call" | custom-call | tf_op jit(solution)/shard_map/pallas_call | solution.py:458

commit v7 on v3

--- a/solution.py
+++ b/solution.py
@@ -10,14 +10,16 @@
 
 EPS_COUNT = 1e-6
 ALPHA = 1e-3
+PIECES = 8
 LOG2E = math.log2(math.e)
 LN2 = math.log(2.0)
-KB = 512
+KB = 1024
 IB = 256
-KT = 64
+KT = 512
 MB = 1024
 EARLY = 3
-FB = 256
+SB = 256
+FB = 512
 MESH = pl.DeviceIdType.MESH
 F32 = jnp.float32
 BF16 = jnp.bfloat16
@@ -34,6 +36,7 @@
     n_kt = own // KT
     n_mb = own // MB
     n_fb = own // FB
+    n_sb = own // SB
     n_ch = nq // IB
     fit = lax.axis_index("fit")
     comp = lax.axis_index("comp")
@@ -102,26 +105,36 @@
 
     lax.fori_loop(0, n_kb, init_body, 0)
 
-    def e_tile(i0, tb):
-        cols = pl.ds(pl.multiple_of(i0, IB), IB)
-        xt = x_ref[cols, :]
-        for kb in range(n_kb):
+    def e_tiles(starts, tb):
+        def logits(i0, kb):
+            xt = x_ref[pl.ds(pl.multiple_of(i0, IB), IB), :]
             a = lax.dot_general(mub_ref[pl.ds(kb * KB, KB), :], xt, NT, preferred_element_type=F32)
             for u in range(KB // KT):
-                rows = pl.ds(kb * KB + u * KT, KT)
-                tile = kb * (KB // KT) + u
-                cc = c_ref[rows, :]
+                cc = c_ref[pl.ds(kb * KB + u * KT, KT), :]
                 l = a[u * KT:(u + 1) * KT, :] * tb + jnp.concatenate([cc, cc], axis=1)
-                l3 = l.reshape(KT // 8, 8, IB)
-                m = jnp.max(l3, axis=0)
-                p3 = jnp.exp2(l3 - m[None])
+                yield kb * (KB // KT) + u, pl.ds(kb * KB + u * KT, KT), l.reshape(KT // 8, 8, IB)
+
+        def maxima(i0, kb):
+            cols = pl.ds(pl.multiple_of(i0, IB), IB)
+            for tile, _, l3 in logits(i0, kb):
+                m_ref[tile, :, cols] = jnp.max(l3, axis=0)
+
+        def exponentials(i0, kb):
+            cols = pl.ds(pl.multiple_of(i0, IB), IB)
+            for tile, rows, l3 in logits(i0, kb):
+                p3 = jnp.exp2(l3 - m_ref[tile, :, cols][None])
                 p_ref[rows, cols] = p3.reshape(KT, IB)
-                m_ref[tile, :, cols] = m
                 sum_ref[tile, :, cols] = jnp.sum(p3, axis=0)
 
+        steps = [(i0, kb) for i0 in starts for kb in range(n_kb)]
+        maxima(*steps[0])
+        for i, step in enumerate(steps):
+            if i + 1 < len(steps):
+                maxima(*steps[i + 1])
+            exponentials(*step)
+
     def e_quarter(q, tb):
-        for it in range(n_ch):
-            e_tile(q * nq + it * IB, tb)
+        e_tiles([q * nq + it * IB for it in range(n_ch)], tb)
 
     def st_copy(t, q, r):
         return pltpu.make_async_remote_copy(
@@ -131,9 +144,7 @@
     def st_send_all(t, q):
         cols = pl.ds(pl.multiple_of(q * nq, nq), nq)
         top = jnp.max(jnp.max(m_ref[:, :, cols], axis=0), axis=0, keepdims=True)
-        part = [pl.ds(k, 8) for k in range(0, n_kt, 8)]
-        tot = functools.reduce(lambda u, v: u + v,
-                               [jnp.sum(sum_ref[k, :, cols] * jnp.exp2(m_ref[k, :, cols] - top), axis=0) for k in part])
+        tot = jnp.sum(sum_ref[:, :, cols] * jnp.exp2(m_ref[:, :, cols] - top), axis=0)
         tot = jnp.sum(tot, axis=0, keepdims=True)
         g_ref[t, q, me] = top + LOG2E * jnp.log(tot)
         for r in range(1, 8):
@@ -180,14 +191,14 @@
         return n, mu
 
     def mu_copy(j):
-        rows = pl.ds(pl.multiple_of(j * FB, FB), FB)
+        rows = pl.ds(pl.multiple_of(j * SB, SB), SB)
         return pltpu.make_async_remote_copy(
             src_ref=mub_ref.at[rows], dst_ref=muf_ref.at[rows], send_sem=mu_send.at[j], recv_sem=mu_recv.at[j],
             device_id=peer(2), device_id_type=MESH)
 
     def c_copy():
         return pltpu.make_async_remote_copy(
-            src_ref=crow_ref, dst_ref=cfrow_ref, send_sem=mu_send.at[n_fb], recv_sem=mu_recv.at[n_fb],
+            src_ref=crow_ref, dst_ref=cfrow_ref, send_sem=mu_send.at[n_sb], recv_sem=mu_recv.at[n_sb],
             device_id=peer(2), device_id_type=MESH)
 
     def m_second(kb, beta_next, share):
@@ -238,9 +249,9 @@
             def far_points(ch, _):
                 pts_copy(1, ch).wait_recv()
                 pts_copy(2, ch).start()
-                e_tile(par * nq + ch * IB, tb)
+                e_tiles([par * nq + ch * IB], tb)
                 pts_copy(2, ch).wait_recv()
-                e_tile(data_xor(3) * nq + ch * IB, tb)
+                e_tiles([data_xor(3) * nq + ch * IB], tb)
                 return 0
 
             lax.fori_loop(0, n_ch, far_points, 0)
@@ -249,7 +260,7 @@
         else:
             lax.fori_loop(0, 4, lambda s, _: (e_step(t, (s % 2) * 2 + s // 2, tb), 0)[1], 0)
             if last:
-                for j in range(EARLY, n_fb):
+                for j in range(EARLY, n_sb):
                     mu_copy(j).start()
         st_combine(t, 0)
         st_combine(t, 2)
@@ -276,7 +287,8 @@
             c_copy().wait_recv()
 
             def far_block(kb, _):
-                mu_copy(kb).wait_recv()
+                for j in range(FB // SB):
+                    mu_copy(kb * (FB // SB) + j).wait_recv()
                 rows = pl.ds(pl.multiple_of(kb * FB, FB), FB)
                 c = to_col(cfrow_ref[:, rows])
                 c2 = jnp.concatenate([c, c], axis=1)
@@ -311,7 +323,7 @@
         for q in range(4):
             for r in range(1, 8):
                 st_copy(t, q, r).wait_send()
-    for j in range(n_fb):
+    for j in range(n_sb):
         mu_copy(j).wait_send()
     c_copy().wait_send()
     for slot in range(2):
@@ -333,6 +345,18 @@
 
     sibling(0)
     sibling(1)
+
+
+def flush_kernel(means_ref, logw_ref, lse_ref, means_out, logw_out, lse_out, sem):
+    rows = means_ref.shape[0] // PIECES
+    copies = [pltpu.make_async_copy(means_ref.at[pl.ds(i * rows, rows)], means_out.at[pl.ds(i * rows, rows)], sem.at[i])
+              for i in range(PIECES)]
+    copies.append(pltpu.make_async_copy(logw_ref, logw_out, sem.at[PIECES]))
+    copies.append(pltpu.make_async_copy(lse_ref, lse_out, sem.at[PIECES + 1]))
+    for cp in copies:
+        cp.start()
+    for cp in copies:
+        cp.wait()
 
 
 def solution(mesh):
@@ -351,7 +375,7 @@
         any_spec = pl.BlockSpec(memory_space=pl.ANY)
         vmem_spec = pl.BlockSpec(memory_space=pltpu.VMEM)
         dma = pltpu.SemaphoreType.DMA
-        n_fb = own // FB
+        n_fb, n_sb = own // FB, own // SB
         means, logw, lse = pl.pallas_call(
             functools.partial(fit_kernel, cfg),
             out_shape=(pltpu.VMEM((rows, dim), F32),
@@ -376,13 +400,22 @@
                 dma((3,)),
                 dma((3, nq // IB)), dma((3, nq // IB)),
                 dma((sweeps, 4, 8)), dma((sweeps, 4, 8)),
-                dma((n_fb + 1,)), dma((n_fb + 1,)),
+                dma((n_sb + 1,)), dma((n_sb + 1,)),
                 dma((2, n_fb)), dma((2, n_fb)),
                 dma((2,)), dma((2,)),
             ],
             compiler_params=pltpu.CompilerParams(
                 collective_id=0, has_side_effects=True, vmem_limit_bytes=54 * 1024 * 1024),
         )(inv_temp, points, mu_init, logpi_init.reshape(data_size, 1, own))
+        results = [pltpu.with_memory_space_constraint(v, pltpu.VMEM) for v in (means, logw, lse)]
+        means, logw, lse = pl.pallas_call(
+            flush_kernel,
+            out_shape=tuple(jax.ShapeDtypeStruct(v.shape, F32) for v in results),
+            in_specs=[vmem_spec] * 3,
+            out_specs=(any_spec,) * 3,
+            scratch_shapes=[dma((PIECES + 2,))],
+            compiler_params=pltpu.CompilerParams(vmem_limit_bytes=16 * 1024 * 1024),
+        )(*results)
         return means, logw.reshape(rows), lse.reshape(nq)
 
     row_spec = P(("fit", "data"), None)

time: 86.8 us -> 84.3 us (0.971)
  local copies, waits for them, and re-layouts: 4.61 us -> 0 us
  Pallas kernels: 81.4 us -> 83.4 us
    unnamed x3 -> x0, local copies, waits for them, and re-layouts: 4.61 us -> none
    pallas_call x0 -> x1, Pallas kernels: none -> 3.39 us  [local_fit(): pl.pallas_call(flush_kernel, out_shape=tuple((jax.ShapeDtypeStruct(v.shap...]
    pallas_call x1, Pallas kernels: 81.4 us -> 80 us  [local_fit(): pl.pallas_call(functools.partial(fit_kernel, cfg), out_shape=(pltpu.VMEM(...]
where the time goes in v7:
time: 84.3 us; the launch traced here: 84.2 us
  Pallas kernels  83.4 us (99%)
    pallas_call x1, Pallas kernels, local_fit(): pl.pallas_call(functools.partial(fit_kernel, cfg), out_shape=(pltpu.VMEM(...  80 us
    pallas_call x1, Pallas kernels, local_fit(): pl.pallas_call(flush_kernel, out_shape=tuple((jax.ShapeDtypeStruct(v.shap...  3.39 us

profile of v7, /device:TPU:0, one launch (start us, length us, event | category | flops | bytes accessed | tf_op | source)
XLA Modules:
  0.0 84.2 jit_solution(6362889083146450491)
XLA Ops:
  0.6 80.0 %shard_map.67 = (f32[8192,256]{1,0:T(8,128)S(1)}, f32[4,1,2048]{2,1,0:T(1,128)S(1)}, f32[1,1024]{1,0:T(1,128)S(1)}) custom-call(f32[3]{0:T(128)} %temp_ref.1, bf16[1024,256]{1,0:T(8,128)(2,1)} %pts_ref.1, f32[8192,256]{1,0:T(8,128)} %mu_ref.1, f32[4,1,2048]{2,1,0:T(1,128)} %bitcast.3), custom_call_target="tpu_custom_call" | custom-call | tf_op jit(solution)/shard_map/pallas_call | solution.py:379
  80.7 3.4 %shard_map.68 = (f32[8192,256]{1,0:T(8,128)}, f32[4,1,2048]{2,1,0:T(1,128)}, f32[1,1024]{1,0:T(1,128)}) custom-call(f32[8192,256]{1,0:T(8,128)S(1)} %get-tuple-element.9.means_ref, f32[4,1,2048]{2,1,0:T(1,128)S(1)} %get-tuple-element.10.logw_ref, f32[1,1024]{1,0:T(1,128)S(1)} %get-tuple-element.11.lse_ref), custom_call_target="tpu_custom_call" | custom-call | tf_op jit(solution)/shard_map/pallas_call | solution.py:411

commit v8 on v7

--- a/solution.py
+++ b/solution.py
@@ -385,7 +385,7 @@
             out_specs=(vmem_spec, vmem_spec, vmem_spec),
             scratch_shapes=[
                 pltpu.VMEM((n_pts, dim), BF16),
-                pltpu.VMEM((own, n_pts), F32),
+                pltpu.VMEM((own, n_pts + 128), F32),
                 pltpu.VMEM((own, dim), BF16),
                 pltpu.VMEM((own, dim), BF16),
                 pltpu.VMEM((own, 128), F32),

time: 84.3 us -> 84.2 us (level)
  no operation moved by 1% of the time
where the time goes in v8:
time: 84.2 us; the launch traced here: 84.1 us
  Pallas kernels  83.3 us (99%)
    pallas_call x1, Pallas kernels, local_fit(): pl.pallas_call(functools.partial(fit_kernel, cfg), out_shape=(pltpu.VMEM(...  79.9 us
    pallas_call x1, Pallas kernels, local_fit(): pl.pallas_call(flush_kernel, out_shape=tuple((jax.ShapeDtypeStruct(v.shap...  3.39 us

profile of v8, /device:TPU:0, one launch (start us, length us, event | category | flops | bytes accessed | tf_op | source)
XLA Modules:
  0.0 84.1 jit_solution(5756979424520398788)
XLA Ops:
  0.6 79.9 %shard_map.67 = (f32[8192,256]{1,0:T(8,128)S(1)}, f32[4,1,2048]{2,1,0:T(1,128)S(1)}, f32[1,1024]{1,0:T(1,128)S(1)}) custom-call(f32[3]{0:T(128)} %temp_ref.1, bf16[1024,256]{1,0:T(8,128)(2,1)} %pts_ref.1, f32[8192,256]{1,0:T(8,128)} %mu_ref.1, f32[4,1,2048]{2,1,0:T(1,128)} %bitcast.3), custom_call_target="tpu_custom_call" | custom-call | tf_op jit(solution)/shard_map/pallas_call | solution.py:379
  80.6 3.4 %shard_map.68 = (f32[8192,256]{1,0:T(8,128)}, f32[4,1,2048]{2,1,0:T(1,128)}, f32[1,1024]{1,0:T(1,128)}) custom-call(f32[8192,256]{1,0:T(8,128)S(1)} %get-tuple-element.9.means_ref, f32[4,1,2048]{2,1,0:T(1,128)S(1)} %get-tuple-element.10.logw_ref, f32[1,1024]{1,0:T(1,128)S(1)} %get-tuple-element.11.lse_ref), custom_call_target="tpu_custom_call" | custom-call | tf_op jit(solution)/shard_map/pallas_call | solution.py:411

commit v9 on v8

--- a/solution.py
+++ b/solution.py
@@ -17,17 +17,17 @@
 IB = 256
 KT = 512
 MB = 1024
-EARLY = 3
+EARLY = 4
 SB = 256
 FB = 512
 MESH = pl.DeviceIdType.MESH
 F32 = jnp.float32
 BF16 = jnp.bfloat16
-NT = (((1,), (1,)), ((), ()))
+NN = (((1,), (0,)), ((), ()))
 
 
 def fit_kernel(cfg, temp_ref, pts_ref, mu_ref, logpi_ref, means_ref, logw_ref, lse_out_ref,
-               x_ref, p_ref, mub_ref, muf_ref, c_ref, crow_ref, cfrow_ref, s_ref, n_ref,
+               x_ref, xt_ref, p_ref, mub_ref, muf_ref, c_ref, crow_ref, cfrow_ref, s_ref, n_ref,
                m_ref, sum_ref, lse_ref, g_ref,
                loc_sem, pts_send, pts_recv, st_send, st_recv, mu_send, mu_recv,
                out_send, out_recv, w_send, w_recv):
@@ -105,10 +105,10 @@
 
     lax.fori_loop(0, n_kb, init_body, 0)
 
-    def e_tiles(starts, tb):
+    def e_tiles(starts, tb, first=False):
         def logits(i0, kb):
-            xt = x_ref[pl.ds(pl.multiple_of(i0, IB), IB), :]
-            a = lax.dot_general(mub_ref[pl.ds(kb * KB, KB), :], xt, NT, preferred_element_type=F32)
+            xt = xt_ref[:, pl.ds(pl.multiple_of(i0, IB), IB)]
+            a = lax.dot_general(mub_ref[pl.ds(kb * KB, KB), :], xt, NN, preferred_element_type=F32)
             for u in range(KB // KT):
                 cc = c_ref[pl.ds(kb * KB + u * KT, KT), :]
                 l = a[u * KT:(u + 1) * KT, :] * tb + jnp.concatenate([cc, cc], axis=1)
@@ -126,6 +126,10 @@
                 p_ref[rows, cols] = p3.reshape(KT, IB)
                 sum_ref[tile, :, cols] = jnp.sum(p3, axis=0)
 
+        if first:
+            for i0 in starts:
+                cols = pl.ds(pl.multiple_of(i0, IB), IB)
+                xt_ref[:, cols] = jnp.transpose(x_ref[cols, :])
         steps = [(i0, kb) for i0 in starts for kb in range(n_kb)]
         maxima(*steps[0])
         for i, step in enumerate(steps):
@@ -133,8 +137,8 @@
                 maxima(*steps[i + 1])
             exponentials(*step)
 
-    def e_quarter(q, tb):
-        e_tiles([q * nq + it * IB for it in range(n_ch)], tb)
+    def e_quarter(q, tb, first):
+        e_tiles([q * nq + it * IB for it in range(n_ch)], tb, first)
 
     def st_copy(t, q, r):
         return pltpu.make_async_remote_copy(
@@ -151,7 +155,7 @@
             st_copy(t, q, r).start()
 
     def e_step(t, q, tb):
-        e_quarter(q, tb)
+        e_quarter(q, tb, t == 0)
         st_send_all(t, q)
 
     def st_combine(t, q):
@@ -249,9 +253,9 @@
             def far_points(ch, _):
                 pts_copy(1, ch).wait_recv()
                 pts_copy(2, ch).start()
-                e_tiles([par * nq + ch * IB], tb)
+                e_tiles([par * nq + ch * IB], tb, True)
                 pts_copy(2, ch).wait_recv()
-                e_tiles([data_xor(3) * nq + ch * IB], tb)
+                e_tiles([data_xor(3) * nq + ch * IB], tb, True)
                 return 0
 
             lax.fori_loop(0, n_ch, far_points, 0)
@@ -296,25 +300,19 @@
                 acc = jnp.zeros((FB, dim), F32)
                 for ic in range(4 * n_ch):
                     cols = pl.ds(ic * IB, IB)
-                    xt = x_ref[cols, :]
-                    a = lax.dot_general(muf_ref[rows, :], xt, NT, preferred_element_type=F32)
+                    a = lax.dot_general(muf_ref[rows, :], xt_ref[:, cols], NN, preferred_element_type=F32)
                     r = jnp.exp2((a * tb + c2) - lse_ref[:, cols])
                     n_acc = n_acc + (r[:, :128] + r[:, 128:])
-                    acc = acc + jnp.dot(r.astype(BF16), xt, preferred_element_type=F32)
+                    acc = acc + jnp.dot(r.astype(BF16), x_ref[cols, :], preferred_element_type=F32)
                 emit(1, kb, n_acc, acc)
                 return 0
 
             lax.fori_loop(0, n_fb, far_block, 0)
             w_copy(1).start()
             mine = pl.ds(pl.multiple_of(data * nq, nq), nq)
-            xo = x_ref[mine, :].astype(F32)
-            sq = xo * xo
-            hi = sq.astype(BF16)
-            lo = (sq - hi.astype(F32)).astype(BF16)
-            ones = jnp.ones((8, dim), BF16)
-            row_sq = (lax.dot_general(ones, hi, NT, preferred_element_type=F32)
-                      + lax.dot_general(ones, lo, NT, preferred_element_type=F32))
-            lse_out_ref[...] = LN2 * lse_ref[:, mine] - beta * row_sq[0:1, :]
+            xo = xt_ref[:, mine].astype(F32)
+            row_sq = jnp.sum(xo * xo, axis=0, keepdims=True)
+            lse_out_ref[...] = LN2 * lse_ref[:, mine] - beta * row_sq
 
     for kind in range(3):
         for ch in range(n_ch):
@@ -385,6 +383,7 @@
             out_specs=(vmem_spec, vmem_spec, vmem_spec),
             scratch_shapes=[
                 pltpu.VMEM((n_pts, dim), BF16),
+                pltpu.VMEM((dim, n_pts), BF16),
                 pltpu.VMEM((own, n_pts + 128), F32),
                 pltpu.VMEM((own, dim), BF16),
                 pltpu.VMEM((own, dim), BF16),

time: 84.2 us -> 85.6 us (1.017)
  Pallas kernels: 83.3 us -> 84.7 us
    pallas_call x1, Pallas kernels: 79.9 us -> 81.3 us  [local_fit(): pl.pallas_call(functools.partial(fit_kernel, cfg), out_shape=(pltpu.VMEM(...]
where the time goes in v9:
time: 85.6 us; the launch traced here: 85.5 us
  Pallas kernels  84.7 us (99%)
    pallas_call x1, Pallas kernels, local_fit(): pl.pallas_call(functools.partial(fit_kernel, cfg), out_shape=(pltpu.VMEM(...  81.3 us
    pallas_call x1, Pallas kernels, local_fit(): pl.pallas_call(flush_kernel, out_shape=tuple((jax.ShapeDtypeStruct(v.shap...  3.39 us

profile of v9, /device:TPU:0, one launch (start us, length us, event | category | flops | bytes accessed | tf_op | source)
XLA Modules:
  0.0 85.5 jit_solution(15700988587901883448)
XLA Ops:
  0.6 81.3 %shard_map.67 = (f32[8192,256]{1,0:T(8,128)S(1)}, f32[4,1,2048]{2,1,0:T(1,128)S(1)}, f32[1,1024]{1,0:T(1,128)S(1)}) custom-call(f32[3]{0:T(128)} %temp_ref.1, bf16[1024,256]{1,0:T(8,128)(2,1)} %pts_ref.1, f32[8192,256]{1,0:T(8,128)} %mu_ref.1, f32[4,1,2048]{2,1,0:T(1,128)} %bitcast.3), custom_call_target="tpu_custom_call" | custom-call | tf_op jit(solution)/shard_map/pallas_call | solution.py:377
  82.0 3.4 %shard_map.68 = (f32[8192,256]{1,0:T(8,128)}, f32[4,1,2048]{2,1,0:T(1,128)}, f32[1,1024]{1,0:T(1,128)}) custom-call(f32[8192,256]{1,0:T(8,128)S(1)} %get-tuple-element.9.means_ref, f32[4,1,2048]{2,1,0:T(1,128)S(1)} %get-tuple-element.10.logw_ref, f32[1,1024]{1,0:T(1,128)S(1)} %get-tuple-element.11.lse_ref), custom_call_target="tpu_custom_call" | custom-call | tf_op jit(solution)/shard_map/pallas_call | solution.py:410

commit v10 on v8

--- a/solution.py
+++ b/solution.py
@@ -246,17 +246,18 @@
                 pts_copy(0, ch).wait_recv()
             lax.fori_loop(0, 2, lambda s, _: (e_step(0, xpos * 2 + s, tb), 0)[1], 0)
 
+            away = (1 - xpos) * 2
+
             def far_points(ch, _):
                 pts_copy(1, ch).wait_recv()
                 pts_copy(2, ch).start()
-                e_tiles([par * nq + ch * IB], tb)
                 pts_copy(2, ch).wait_recv()
-                e_tiles([data_xor(3) * nq + ch * IB], tb)
+                e_tiles([away * nq + ch * IB], tb)
                 return 0
 
             lax.fori_loop(0, n_ch, far_points, 0)
-            st_send_all(0, par)
-            st_send_all(0, data_xor(3))
+            st_send_all(0, away)
+            e_step(0, away + 1, tb)
         else:
             lax.fori_loop(0, 4, lambda s, _: (e_step(t, (s % 2) * 2 + s // 2, tb), 0)[1], 0)
             if last:

time: 84.2 us -> 83.7 us (level)
  no operation moved by 1% of the time
where the time goes in v10:
time: 83.7 us; the launch traced here: 83.6 us
  Pallas kernels  82.8 us (99%)
    pallas_call x1, Pallas kernels, local_fit(): pl.pallas_call(functools.partial(fit_kernel, cfg), out_shape=(pltpu.VMEM(...  79.4 us
    pallas_call x1, Pallas kernels, local_fit(): pl.pallas_call(flush_kernel, out_shape=tuple((jax.ShapeDtypeStruct(v.shap...  3.39 us

profile of v10, /device:TPU:0, one launch (start us, length us, event | category | flops | bytes accessed | tf_op | source)
XLA Modules:
  0.0 83.6 jit_solution(6067561158595415749)
XLA Ops:
  0.6 79.4 %shard_map.67 = (f32[8192,256]{1,0:T(8,128)S(1)}, f32[4,1,2048]{2,1,0:T(1,128)S(1)}, f32[1,1024]{1,0:T(1,128)S(1)}) custom-call(f32[3]{0:T(128)} %temp_ref.1, bf16[1024,256]{1,0:T(8,128)(2,1)} %pts_ref.1, f32[8192,256]{1,0:T(8,128)} %mu_ref.1, f32[4,1,2048]{2,1,0:T(1,128)} %bitcast.3), custom_call_target="tpu_custom_call" | custom-call | tf_op jit(solution)/shard_map/pallas_call | solution.py:380
  80.0 3.4 %shard_map.68 = (f32[8192,256]{1,0:T(8,128)}, f32[4,1,2048]{2,1,0:T(1,128)}, f32[1,1024]{1,0:T(1,128)}) custom-call(f32[8192,256]{1,0:T(8,128)S(1)} %get-tuple-element.9.means_ref, f32[4,1,2048]{2,1,0:T(1,128)S(1)} %get-tuple-element.10.logw_ref, f32[1,1024]{1,0:T(1,128)S(1)} %get-tuple-element.11.lse_ref), custom_call_target="tpu_custom_call" | custom-call | tf_op jit(solution)/shard_map/pallas_call | solution.py:412

commit v11 on v10

--- a/solution.py
+++ b/solution.py
@@ -248,14 +248,22 @@
 
             away = (1 - xpos) * 2
 
-            def far_points(ch, _):
+            def pass_on(ch):
                 pts_copy(1, ch).wait_recv()
                 pts_copy(2, ch).start()
+
+            def take(ch):
                 pts_copy(2, ch).wait_recv()
                 e_tiles([away * nq + ch * IB], tb)
+
+            def far_points(ch, _):
+                pass_on(ch + 1)
+                take(ch)
                 return 0
 
-            lax.fori_loop(0, n_ch, far_points, 0)
+            pass_on(0)
+            lax.fori_loop(0, n_ch - 1, far_points, 0)
+            take(n_ch - 1)
             st_send_all(0, away)
             e_step(0, away + 1, tb)
         else:

time: 83.7 us -> 84 us (level)
  no operation moved by 1% of the time
where the time goes in v11:
time: 84 us; the launch traced here: 83.9 us
  Pallas kernels  83.1 us (99%)
    pallas_call x1, Pallas kernels, local_fit(): pl.pallas_call(functools.partial(fit_kernel, cfg), out_shape=(pltpu.VMEM(...  79.7 us
    pallas_call x1, Pallas kernels, local_fit(): pl.pallas_call(flush_kernel, out_shape=tuple((jax.ShapeDtypeStruct(v.shap...  3.39 us

profile of v11, /device:TPU:0, one launch (start us, length us, event | category | flops | bytes accessed | tf_op | source)
XLA Modules:
  0.0 83.9 jit_solution(18425423402671854221)
XLA Ops:
  0.6 79.7 %shard_map.67 = (f32[8192,256]{1,0:T(8,128)S(1)}, f32[4,1,2048]{2,1,0:T(1,128)S(1)}, f32[1,1024]{1,0:T(1,128)S(1)}) custom-call(f32[3]{0:T(128)} %temp_ref.1, bf16[1024,256]{1,0:T(8,128)(2,1)} %pts_ref.1, f32[8192,256]{1,0:T(8,128)} %mu_ref.1, f32[4,1,2048]{2,1,0:T(1,128)} %bitcast.3), custom_call_target="tpu_custom_call" | custom-call | tf_op jit(solution)/shard_map/pallas_call | solution.py:388
  80.3 3.4 %shard_map.68 = (f32[8192,256]{1,0:T(8,128)}, f32[4,1,2048]{2,1,0:T(1,128)}, f32[1,1024]{1,0:T(1,128)}) custom-call(f32[8192,256]{1,0:T(8,128)S(1)} %get-tuple-element.9.means_ref, f32[4,1,2048]{2,1,0:T(1,128)S(1)} %get-tuple-element.10.logw_ref, f32[1,1024]{1,0:T(1,128)S(1)} %get-tuple-element.11.lse_ref), custom_call_target="tpu_custom_call" | custom-call | tf_op jit(solution)/shard_map/pallas_call | solution.py:420
